TPU v7x, 32 devices: a whole 2x2x4 slice. The times are simulated.
32 devices in a mesh: trans: 16 (over z, y, x), los: 2 (over core).
Axes of the slice: x: 2, y: 2, z: 4, core: 2. Of those that a mesh axis runs over, the one named last changes fastest.
Arguments:
- density: bfloat16 [2, 2048, 2048], P('los', 'trans'), may hold values from -6 to 6
- row_pos: float32 [2, 2048], replicated, may hold values from 0 to 2048
- col_pos: float32 [2, 2048], replicated, may hold values from 0 to 2048
- plane_of_slot: int32 [2], replicated, may hold values from 0 to 1, each once
- plane_bin: int32 [2], replicated, may hold values from 0 to 3, as said below
- efficiency: float32 [4, 2], replicated, may hold values from 0.3 to 3
Outputs:
- shear: float32 [2, 4, 2048, 2048], P(None, None, ('trans', 'los'))
Inputs may be any that keep to these rules, and one draw needn't show every extreme that they name: `plane_bin`: some plane has bin 0 and some plane has bin 4 - 1.
All inputs are finite; a program needn't handle non-finite values.
Results may differ from a plain program's by a relative error of at most 0.006.
Values may be sent and summed in bfloat16 or wider, within the bound.
A program may use at most 64 MiB of HBM per device.

v0:
```python
import math

import jax
import jax.numpy as jnp
from jax import lax
from jax.sharding import PartitionSpec as P


def hat_block(positions, mesh_cells):
    cells = jnp.arange(mesh_cells, dtype=jnp.int32).astype(jnp.float32)
    offset = positions[:, None] - cells[None, :] + 0.5 * mesh_cells
    folded = jnp.mod(offset, 1.0 * mesh_cells) - 0.5 * mesh_cells
    return jnp.maximum(1.0 - jnp.abs(folded), 0.0).astype(jnp.bfloat16)


def trig_pair(rows_n, cols_n, modulus, sign_value):
    product_index = (
        jnp.arange(rows_n, dtype=jnp.int32)[:, None]
        * jnp.arange(cols_n, dtype=jnp.int32)[None, :]
        % modulus
    )
    angle = product_index.astype(jnp.float32) * (2.0 * math.pi / modulus)
    return (jnp.cos(angle), sign_value * jnp.sin(angle))


def fourier(real_part, imag_part, inverse):
    length = real_part.shape[-1]
    factor_one = 16
    second = length // factor_one
    sign_value = 1.0 if inverse else -1.0
    lead_shape = real_part.shape[:-1]
    highest = lax.Precision.HIGHEST
    cos_one, sin_one = trig_pair(factor_one, factor_one, factor_one, sign_value)
    real_grid = real_part.reshape(lead_shape + (factor_one, second))
    imag_grid = imag_part.reshape(lead_shape + (factor_one, second))

    def first_pass(table, values):
        return jnp.einsum("kn,...nm->...km", table, values, precision=highest)

    section_real = first_pass(cos_one, real_grid) - first_pass(sin_one, imag_grid)
    section_imag = first_pass(cos_one, imag_grid) + first_pass(sin_one, real_grid)
    cos_twid, sin_twid = trig_pair(factor_one, second, length, sign_value)
    turned_real = section_real * cos_twid - section_imag * sin_twid
    turned_imag = section_real * sin_twid + section_imag * cos_twid
    cos_two, sin_two = trig_pair(second, second, second, sign_value)

    def second_pass(values, table):
        return jnp.einsum("...km,mj->...kj", values, table, precision=highest)

    out_real = second_pass(turned_real, cos_two) - second_pass(turned_imag, sin_two)
    out_imag = second_pass(turned_real, sin_two) + second_pass(turned_imag, cos_two)
    out_real = jnp.swapaxes(out_real, -1, -2).reshape(lead_shape + (length,))
    out_imag = jnp.swapaxes(out_imag, -1, -2).reshape(lead_shape + (length,))
    scale = 1.0 / length if inverse else 1.0
    return (out_real * scale, out_imag * scale)


def wave_numbers(index_all, length):
    return jnp.where(index_all < length // 2, index_all, index_all - length).astype(jnp.float32)


def body(density, row_pos, col_pos, plane_of_slot, plane_bin, efficiency):
    count_trans = lax.axis_size("trans")
    count_los = lax.axis_size("los")
    per_device = density.shape[0]
    mesh_cells = density.shape[2]
    grid_cells = row_pos.shape[1]
    planes_total = row_pos.shape[0]
    bins_total = efficiency.shape[0]
    width_cols = grid_cells // (count_trans * count_los)
    block_rows = min(512, grid_cells)
    slots = jnp.arange(planes_total, dtype=jnp.int32)
    bin_index = jnp.arange(bins_total, dtype=jnp.int32)
    by_columns = lax.all_to_all(density, "trans", split_axis=2, concat_axis=1, tiled=True)
    local_slot = 0
    slot_now = lax.axis_index("los") * per_device + local_slot
    plane_id = jnp.sum(jnp.where(slots == slot_now, plane_of_slot, 0))
    chosen = slots == plane_id
    plane_eff = jnp.sum(jnp.where(chosen[None, :], efficiency, 0.0), axis=1)
    first_bin = jnp.sum(jnp.where(chosen, plane_bin, 0))
    weight_list = [plane_eff * (bin_index >= first_bin).astype(jnp.float32)]
    rows_here = jnp.sum(jnp.where(chosen[:, None], row_pos, 0.0), axis=0)
    cols_here = jnp.sum(jnp.where(chosen[:, None], col_pos, 0.0), axis=0)
    pieces = []
    for begin in range(0, grid_cells, block_rows):
        row_block = hat_block(rows_here[begin : begin + block_rows], mesh_cells)
        pieces.append(
            lax.dot_general(
                by_columns[local_slot],
                row_block,
                (((0,), (1,)), ((), ())),
                preferred_element_type=jnp.float32,
            )
        )
    resampled = [jnp.concatenate(pieces, axis=1).astype(jnp.bfloat16)]
    col_tables = [hat_block(cols_here, mesh_cells)]
    half_columns = jnp.stack(resampled)
    exchanged = lax.all_to_all(half_columns, "trans", split_axis=2, concat_axis=1, tiled=True)
    local_slot = 0
    rows_map = lax.dot_general(
        exchanged[local_slot],
        col_tables[local_slot],
        (((0,), (1,)), ((), ())),
        preferred_element_type=jnp.float32,
    )
    plane_term = weight_list[local_slot][None, :, None] * rows_map[:, None, :]
    term_real, term_imag = fourier(plane_term, jnp.zeros_like(plane_term), False)
    summed_real, summed_imag = (
        lax.psum_scatter(term_real, "los", scatter_dimension=2, tiled=True),
        lax.psum_scatter(term_imag, "los", scatter_dimension=2, tiled=True),
    )
    arrived = lax.all_to_all(
        jnp.stack([summed_real, summed_imag]), "trans", split_axis=3, concat_axis=1, tiled=True
    )
    columns_local = arrived.transpose(0, 2, 3, 1)
    col_index = (
        lax.axis_index("los") * (grid_cells // count_los)
        + lax.axis_index("trans") * width_cols
        + jnp.arange(width_cols, dtype=jnp.int32)
    )
    freq_real, freq_imag = fourier(columns_local[0], columns_local[1], False)
    wave_rows = wave_numbers(jnp.arange(grid_cells, dtype=jnp.int32), grid_cells)[None, :]
    wave_cols = wave_numbers(col_index, grid_cells)[:, None]
    square_sum = jnp.maximum(wave_rows * wave_rows + wave_cols * wave_cols, 1.0)
    first_factor = (wave_rows * wave_rows - wave_cols * wave_cols) / square_sum
    second_factor = 2.0 * wave_rows * wave_cols / square_sum
    kernel_real = first_factor * freq_real - second_factor * freq_imag
    kernel_imag = first_factor * freq_imag + second_factor * freq_real
    back_real, back_imag = fourier(kernel_real, kernel_imag, True)
    returned = jnp.stack([back_real, back_imag]).transpose(0, 3, 1, 2)
    rows_local = lax.all_to_all(
        lax.all_to_all(returned, "trans", split_axis=1, concat_axis=3, tiled=True),
        "los",
        split_axis=1,
        concat_axis=3,
        tiled=True,
    )
    final_real, final_imag = fourier(rows_local[0], rows_local[1], True)
    return jnp.stack([final_real, final_imag]).transpose(0, 2, 1, 3)


def solution(mesh):
    placed = (P("los", "trans", None), P(), P(), P(), P(), P())
    return jax.shard_map(
        body,
        mesh=mesh,
        in_specs=placed,
        out_specs=P(None, None, ("trans", "los"), None),
        check_vma=False,
    )
```

profile of v0, /device:TPU:0, one launch (start us, length us, event | category | flops | bytes accessed | tf_op | source)
XLA Modules:
  0.0 628.0 jit_solution(389081637381458077)
XLA Ops:
  9.4 11.4 %reduce = bf16[2048,128]{1,0:T(8,128)(2,1)S(1)} reduce(bf16[2048,1,128]{2,1,0:T(2,128)(2,1)S(1)} %bitcast.333, bf16[]{:T(256)} %broadcast.788), dimensions={1}, to_apply=%bitcast.274.reduce_sub_computation | reduce | bytes 1048578
  21.8 8.9 %all-to-all-start = ((bf16[16,2,8192]{2,1,0:T(2,128)(2,1)}), bf16[16,2,8192]{2,1,0:T(2,128)(2,1)S(1)}, u32[]{:S(2)}, u32[]{:S(2)}) async-start(bf16[16,2,8192]{2,1,0:T(2,128)(2,1)} %reshape.416), calls=%async_computation | async-start | bytes 1048576 | tf_op jit(solution)/shard_map/all_to_all | solution.py:74
  32.2 13.6 %all-to-all-done = bf16[16,2,8192]{2,1,0:T(2,128)(2,1)S(1)} async-done(((bf16[16,2,8192]{2,1,0:T(2,128)(2,1)}), bf16[16,2,8192]{2,1,0:T(2,128)(2,1)S(1)}, u32[]{:S(2)}, u32[]{:S(2)}) %all-to-all-start) | async-done | bytes 524320 | tf_op jit(solution)/shard_map/all_to_all | solution.py:74
  46.6 3.8 fusion.108
  50.4 3.8 fusion.111
  54.2 3.8 fusion.114
  57.9 3.8 fusion.117
  61.7 8.1 %copy.182 = bf16[1,128,2048]{1,0,2:T(2,128)(2,1)S(1)} copy(bf16[1,128,2048]{1,2,0:T(8,128)(2,1)S(1)} %pad_maximum_fusion.1) | data formatting | bytes 1048576 | tf_op jit(solution)/shard_map/concatenate | solution.py:95
  69.9 11.6 %reduce.1 = bf16[2048,128]{1,0:T(8,128)(2,1)S(1)} reduce(bf16[2048,1,128]{2,1,0:T(2,128)(2,1)S(1)} %bitcast.334, bf16[]{:T(256)} %broadcast.788), dimensions={1}, to_apply=%bitcast.300.reduce_sub_computation | reduce | bytes 1048578
  82.4 4.0 all-to-all-start.1
  88.5 12.4 %all-to-all-done.1 = bf16[16,2,8192]{2,1,0:T(2,128)(2,1)S(1)} async-done(((bf16[16,2,8192]{2,1,0:T(2,128)(2,1)}), bf16[16,2,8192]{2,1,0:T(2,128)(2,1)S(1)}, u32[]{:S(2)}, u32[]{:S(2)}) %all-to-all-start.1) | async-done | bytes 524320 | tf_op jit(solution)/shard_map/all_to_all | solution.py:98
  102.0 12.7 %fusion.8 = f32[128,16,128]{2,0,1:T(8,128)S(1)} fusion(bf16[2048,128,1]{0,1,2:T(8,128)(2,1)S(1)} %reshape.400, f32[2048]{0:T(1024)S(1)} %iota_convert_fusion, f32[16,128]{1,0:T(8,128)S(1)} %bitcast.343), kind=kOutput, calls=%fused_computation.12 | convolution fusion | flops 1128267776 | bytes 1589248 | tf_op jit(solution)/shard_map/dot_general | solution.py:100
  115.4 4.1 fusion.12
  119.5 3.9 fusion.10
  125.3 3.2 fusion.36
  128.5 6.5 %fusion.52 = f32[128,4,16,128]{0,3,2,1:T(8,128)S(1)} fusion(f32[128,4,16,128]{3,2,1,0:T(8,128)S(1)} %get-tuple-element.10), kind=kOutput, calls=%fused_computation.75 | convolution fusion | flops 1610858496 | bytes 8388608 | tf_op jit(solution)/shard_map/...km,mj->...kj/dot_general | solution.py:48
  135.1 6.7 %subtract_bitcast_fusion = f32[128,4,128,16]{0,2,3,1:T(8,128)S(1)} fusion(f32[128,4,16,128]{0,3,2,1:T(8,128)S(1)} %fusion.52, f32[128,4,16,128]{3,2,1,0:T(8,128)S(1)} %get-tuple-element.9), kind=kOutput, calls=%fused_computation.56 | convolution fusion | flops 1611890688 | bytes 12582912 | tf_op jit(solution)/shard_map/...km,mj->...kj/dot_general | solution.py:48
  141.8 4.4 copy.117
  146.2 9.4 %fusion.50 = f32[128,4,16,128]{0,3,2,1:T(8,128)S(1)} fusion(f32[128,4,16,128]{3,2,1,0:T(8,128)} %copy-done.5), kind=kOutput, calls=%fused_computation.73 | convolution fusion | flops 1610842112 | bytes 8388608 | tf_op jit(solution)/shard_map/...km,mj->...kj/dot_general | solution.py:48
  155.7 6.5 %add_bitcast_fusion = f32[128,4,128,16]{0,2,3,1:T(8,128)S(1)} fusion(f32[128,4,16,128]{0,3,2,1:T(8,128)S(1)} %fusion.50, f32[128,4,16,128]{3,2,1,0:T(8,128)S(1)} %copy-done.4), kind=kOutput, calls=%fused_computation.55 | convolution fusion | flops 1611907072 | bytes 12582912 | tf_op jit(solution)/shard_map/...km,mj->...kj/dot_general | solution.py:48
  162.2 4.4 copy.122
  166.7 10.4 %reduce-scatter.5.cloned.1.call-done = f32[128,4,1024]{0,2,1:T(8,128)} async-done(((f32[128,4,2048]{0,2,1:T(8,128)}), f32[128,4,1024]{0,2,1:T(8,128)}) %reduce-scatter.5.cloned.1.call-update) | async-done | bytes 2097168 | tf_op jit(solution)/shard_map/reduce_scatter | solution.py:110
  179.7 4.9 copy.123
  184.6 7.0 %all-to-all-start.2 = ((f32[2,128,4,1024]{1,2,0,3:T(4,128)}), f32[2,128,4,1024]{1,2,0,3:T(4,128)}, u32[]{:S(2)}, u32[]{:S(2)}) async-start(f32[2,128,4,1024]{1,2,0,3:T(4,128)} %copy.123), calls=%async_computation.4 | async-start | bytes 8388608 | tf_op jit(solution)/shard_map/all_to_all | solution.py:112
  193.2 78.7 %all-to-all-done.2 = f32[2,128,4,1024]{1,2,0,3:T(4,128)} async-done(((f32[2,128,4,1024]{1,2,0,3:T(4,128)}), f32[2,128,4,1024]{1,2,0,3:T(4,128)}, u32[]{:S(2)}, u32[]{:S(2)}) %all-to-all-start.2) | async-done | bytes 4194336 | tf_op jit(solution)/shard_map/all_to_all | solution.py:112
  271.9 3.0 copy.124
  284.6 2.6 fusion.125
  287.2 3.4 fusion.123
  290.6 3.5 subtract_bitcast_fusion.1
  294.1 4.4 copy.126
  298.5 5.6 add_bitcast_fusion.1
  304.1 4.5 copy.127
  308.6 8.7 %fusion.34 = (f32[4,64,16,128]{1,3,2,0:T(8,128)}, f32[4,64,16,128]{1,3,2,0:T(8,128)}) fusion(f32[64,16,128]{0,2,1:T(8,128)S(1)} %copy-done.15, f32[64,16,128]{0,2,1:T(8,128)S(1)} %get-tuple-element.15, f32[4,64,16,128]{1,3,2,0:T(8,128)} %bitcast.325, f32[4,64,16,128]{1,3,2,0:T(8,128)} %bitcast.323), kind=kLoop, calls=%fused_computation.45 | loop fusion | flops 3145728 | bytes 9437184 | tf_op jit(solution)/shard_map/sub | solution.py:127
  317.4 3.1 copy.128
  320.4 3.3 fusion.208
  323.7 3.2 copy.129
  330.3 3.7 convolution_subtract_fusion.2
  338.1 3.4 fusion.129
  341.6 3.9 multiply_bitcast_fusion.3
  345.5 4.4 copy.132
  349.9 5.6 multiply_bitcast_fusion.2
  355.5 4.4 copy.133
  359.9 4.1 maximum_bitcast_fusion
  364.1 15.3 %copy.181 = f32[2,2048,4,64]{3,2,0,1:T(4,128)} copy(f32[2,2048,4,64]{3,1,2,0:T(8,128)S(1)} %maximum_bitcast_fusion) | data formatting | bytes 8388608 | tf_op jit(solution)/shard_map/transpose | solution.py:130
  379.4 14.6 %reshape.420 = f32[16,1,65536]{2,1,0:T(1,128)} reshape(f32[2048,2,4,64]{3,2,1,0:T(4,128)} %bitcast.312) | data formatting | bytes 8388608
  393.9 113.6 %all_to_all.81 = f32[16,1,65536]{2,1,0:T(1,128)} all-to-all(f32[16,1,65536]{2,1,0:T(1,128)} %reshape.420), channel_id=1, replica_groups=mesh['trans'=16,'los'=2] {'trans'}, dimensions={0} | all-to-all | bytes 8388608 | tf_op jit(solution)/shard_map/all_to_all | solution.py:132
  508.2 13.8 %reduce.2 = f32[16,65536]{1,0:T(8,128)} reduce(f32[16,1,65536]{2,1,0:T(1,128)} %all_to_all.81, f32[]{:T(128)} %broadcast.790), dimensions={1}, to_apply=%all_to_all.69.reduce_sub_computation | reduce | bytes 8388612 | tf_op jit(solution)/shard_map/all_to_all | solution.py:132
  522.0 9.3 %reshape.421 = f32[2048,2,4,64]{3,2,1,0:T(4,128)} reshape(f32[16,65536]{1,0:T(8,128)} %reduce.2) | data formatting | bytes 8388608
  531.2 8.5 %copy.159 = f32[2,16,128,4,64]{2,4,1,3,0:T(8,128)} copy(f32[2,16,128,4,64]{4,3,0,2,1:T(4,128)} %bitcast.311) | data formatting | bytes 8388608 | tf_op jit(solution)/shard_map/all_to_all | solution.py:132
  539.7 5.5 copy.137
  545.3 8.6 %all_to_all.82 = f32[2,128,4,1024]{3,2,0,1:T(4,128)S(1)} all-to-all(f32[2,128,4,1024]{3,2,0,1:T(4,128)} %copy.137), channel_id=1, replica_groups=mesh['trans'=16,'los'=2] {'los'}, dimensions={1} | all-to-all | bytes 8388608 | tf_op jit(solution)/shard_map/all_to_all | solution.py:131
  558.1 2.9 copy.139
  561.1 2.9 reshape_squeeze.14
  564.0 3.3 fusion.204
  567.3 2.9 copy.140
  570.2 3.1 reshape_squeeze.15
  576.7 3.7 convolution_subtract_fusion.1
  584.6 3.4 fusion.135
  588.0 3.8 multiply_bitcast_fusion.1
  591.7 4.8 copy.141
  596.5 5.6 multiply_bitcast_fusion
  602.1 4.8 copy.142
  606.9 7.2 %maximum_bitcast_fusion.1 = f32[2,4,64,2048]{2,3,1,0:T(8,128)} fusion(f32[1,64,4,2048]{1,3,2,0:T(8,128)} %bitcast.328, f32[1,64,4,2048]{1,3,2,0:T(8,128)} %bitcast.324), kind=kLoop, calls=%fused_computation.11 | loop fusion | flops 1048576 | bytes 8388608 | tf_op jit(solution)/shard_map/transpose | solution.py:139
  614.1 6.8 %copy.143 = f32[2,4,64,2048]{3,2,1,0:T(8,128)} copy(f32[2,4,64,2048]{2,3,1,0:T(8,128)} %maximum_bitcast_fusion.1) | data formatting | bytes 8388608 | tf_op jit(solution)/shard_map/transpose | solution.py:139
  (93 shorter events, 46.3 us)
Async XLA Ops:
  8.9 21.8 %copy-start.19 = (s32[2]{0:T(128)S(1)}, s32[2]{0:T(128)}, u32[]{:S(2)}) copy-start(s32[2]{0:T(128)} %param.9) | copy-start | bytes 28
  8.9 23.1 %copy-start.16 = (f32[2,2048]{1,0:T(2,128)S(1)}, f32[2,2048]{1,0:T(2,128)}, u32[]{:S(2)}) copy-start(f32[2,2048]{1,0:T(2,128)} %param.8) | copy-start | bytes 49156
  8.9 23.1 %copy-start.17 = (f32[2,2048]{1,0:T(2,128)S(1)}, f32[2,2048]{1,0:T(2,128)}, u32[]{:S(2)}) copy-start(f32[2,2048]{1,0:T(2,128)} %param.7) | copy-start | bytes 49156
  21.8 23.9 %all-to-all-start = ((bf16[16,2,8192]{2,1,0:T(2,128)(2,1)}), bf16[16,2,8192]{2,1,0:T(2,128)(2,1)S(1)}, u32[]{:S(2)}, u32[]{:S(2)}) async-start(bf16[16,2,8192]{2,1,0:T(2,128)(2,1)} %reshape.416), calls=%async_computation | async-start | bytes 1048576 | tf_op jit(solution)/shard_map/all_to_all | solution.py:74
  69.9 16.6 %copy-start.20 = (s32[2]{0:T(128)S(1)}, s32[2]{0:T(128)}, u32[]{:S(2)}) copy-start(s32[2]{0:T(128)} %param.10) | copy-start | bytes 28
  69.9 17.9 %copy-start.18 = (f32[4,2]{0,1:T(2,128)S(1)}, f32[4,2]{0,1:T(2,128)}, u32[]{:S(2)}) copy-start(f32[4,2]{0,1:T(2,128)} %param.11) | copy-start | bytes 100
  82.4 18.4 %all-to-all-start.1 = ((bf16[16,2,8192]{2,1,0:T(2,128)(2,1)}), bf16[16,2,8192]{2,1,0:T(2,128)(2,1)S(1)}, u32[]{:S(2)}, u32[]{:S(2)}) async-start(bf16[16,2,8192]{2,1,0:T(2,128)(2,1)} %reshape.418), calls=%async_computation.1 | async-start | bytes 1048576 | tf_op jit(solution)/shard_map/all_to_all | solution.py:98
  86.4 80.3 %reduce-scatter.3.cloned.1.call-start = ((), (), s32[]{:S(2)}) async-start(), calls=%async_computation.7 | async-start | bytes 6291456 | tf_op jit(solution)/shard_map/reduce_scatter | solution.py:109
  128.5 6.5 %copy-start.5 = (f32[128,4,16,128]{3,2,1,0:T(8,128)}, f32[128,4,16,128]{3,2,1,0:T(8,128)S(1)}, u32[]{:S(2)}) copy-start(f32[128,4,16,128]{3,2,1,0:T(8,128)S(1)} %get-tuple-element.10) | copy-start | bytes 12582916
  128.5 6.5 %copy-start.3 = (f32[128,4,16,128]{3,2,1,0:T(8,128)}, f32[128,4,16,128]{3,2,1,0:T(8,128)S(1)}, u32[]{:S(2)}) copy-start(f32[128,4,16,128]{3,2,1,0:T(8,128)S(1)} %get-tuple-element.9) | copy-start | bytes 12582916
  146.2 31.0 %reduce-scatter.5.cloned.1.call-start = ((), (), s32[]{:S(2)}) async-start(), calls=%async_computation.8 | async-start | bytes 6291456 | tf_op jit(solution)/shard_map/reduce_scatter | solution.py:110
  146.2 9.5 %copy-start.4 = (f32[128,4,16,128]{3,2,1,0:T(8,128)S(1)}, f32[128,4,16,128]{3,2,1,0:T(8,128)}, u32[]{:S(2)}) copy-start(f32[128,4,16,128]{3,2,1,0:T(8,128)} %copy-done.3) | copy-start | bytes 12582916
  184.6 87.3 %all-to-all-start.2 = ((f32[2,128,4,1024]{1,2,0,3:T(4,128)}), f32[2,128,4,1024]{1,2,0,3:T(4,128)}, u32[]{:S(2)}, u32[]{:S(2)}) async-start(f32[2,128,4,1024]{1,2,0,3:T(4,128)} %copy.123), calls=%async_computation.4 | async-start | bytes 8388608 | tf_op jit(solution)/shard_map/all_to_all | solution.py:112
  284.6 6.0 copy-start.1
  304.1 4.5 copy-start.15
  320.4 3.3 copy-start.6
  327.0 1.3 copy-start.8
  328.3 2.0 copy-start.13
  330.2 3.7 copy-start.7
  336.0 5.6 copy-start.2
  564.0 3.3 copy-start.9
  564.0 3.3 copy-start.14
  573.4 1.3 copy-start.11
  574.7 2.0 copy-start.12
  576.7 3.7 copy-start.10
  582.4 5.6 copy-start
Sparse Core Ops, SparseCore 0:
  146.3 10.2 reduce-scatter.2
  166.8 10.2 reduce-scatter.4
where the time goes:
time: 634 us; the launch traced here: 628 us
  local copies, waits for them, and re-layouts  147 us (23%)
  matrix products  145 us (23%)
  blocking collectives  122 us (19%)
  waiting for transfers between devices  115 us (18%)
  other arithmetic  64.5 us (10%)
  starting transfers between devices  19.9 us (3%)
  between operations  14.4 us (2%)
    all_to_all x1, blocking collectives, body(): lax.all_to_all(returned, 'trans', split_axis=1, concat_axis=3, tiled=True)  114 us
    all_to_all x1, waiting for transfers between devices, body(): lax.all_to_all(jnp.stack([summed_real, summed_imag]), 'trans', split_axis...  78.7 us
    dot_general x16, matrix products, second_pass(): return jnp.einsum('...km,mj->...kj', values, table, precision=highest)  74.2 us
    dot_general x16, matrix products, first_pass(): return jnp.einsum('kn,...nm->...km', table, values, precision=highest)  42.8 us
    unnamed x54, local copies, waits for them, and re-layouts  33.2 us
    unnamed x2, other arithmetic  23.1 us
    mul x4, local copies, waits for them, and re-layouts, fourier(): return (out_real * scale, out_imag * scale)  18.3 us
    transpose x1, local copies, waits for them, and re-layouts, body(): returned = jnp.stack([back_real, back_imag]).transpose(0, 3, 1, 2)  15.3 us
  transfers between devices with their start and end apart: 5, of which 4 were waited for; matrix products, arithmetic and copies ran while one was open for 4% of the time, Pallas kernels for 0%

commit v1 on v0

v1 whole, which is shorter than its diff:
```python
import math

import jax
import jax.numpy as jnp
import numpy as np
from jax import lax
from jax.sharding import PartitionSpec as P

BF = jnp.bfloat16
F32 = jnp.float32
STEP = 32


def slot_layout(length, width):
    half = length // 2
    blocks = half // width
    block = np.arange(2 * half) // (2 * width)
    inner = np.arange(2 * half) % (2 * width)
    is_sine = inner >= width
    member = inner % width
    odd = block >= blocks // 2
    wave = 2 * (np.where(odd, block - blocks // 2, block) * width + member) + odd
    nyquist = is_sine & (wave == 0)
    wave = np.where(nyquist, half, wave)
    phase = np.where(is_sine & ~nyquist, 0.5 * np.pi, 0.0)
    return wave, phase


def small_tables(length, width):
    half = length // 2
    wave, phase = slot_layout(length, width)
    coarse = (np.arange(half // STEP)[:, None] * STEP * wave[None, :]) % length
    fine = (np.arange(STEP)[:, None] * wave[None, :]) % length
    coarse = coarse * (2 * np.pi / length)
    fine = fine * (2 * np.pi / length) + phase[None, :]
    return [np.float32(t) for t in (np.cos(coarse), np.sin(coarse), np.cos(fine), np.sin(fine))]


def full_table(length, width):
    half = length // 2
    cos_a, sin_a, cos_b, sin_b = [jnp.asarray(t) for t in small_tables(length, width)]
    table = cos_a[:, None] * cos_b[None] - sin_a[:, None] * sin_b[None]
    table = table.reshape(half, 2 * half).astype(BF)
    return table[:, :half], table[:, half:]


def hat_rows(positions, cells):
    base = jnp.floor(positions)
    frac = positions - base
    low = base.astype(jnp.int32) % cells
    high = (low + 1) % cells
    index = jnp.arange(cells, dtype=jnp.int32)[None, :]
    value = jnp.where(index == low[:, None], (1.0 - frac)[:, None], 0.0)
    return jnp.where(index == high[:, None], frac[:, None], value).astype(BF)


def dot(a, b, dims):
    return lax.dot_general(a, b, (dims, ((), ())), preferred_element_type=F32)


def lane_waves(length, width, index):
    blocks = length // 2 // width
    lane = lax.broadcasted_iota(jnp.int32, (1, 2 * width), 1)
    is_sine = lane >= width
    member = jnp.where(is_sine, lane - width, lane)
    odd = (index >= blocks // 2).astype(jnp.int32)
    wave = 2 * ((index - odd * (blocks // 2)) * width + member) + odd
    special = is_sine & (wave == 0)
    wave = jnp.where(special, -(length // 2), wave)
    return wave.astype(F32), special, is_sine


def body_plain(density, row_pos, col_pos, plane_of_slot, plane_bin, efficiency):
    count_trans = lax.axis_size("trans")
    count_los = lax.axis_size("los")
    cells = density.shape[2]
    length = row_pos.shape[1]
    half = length // 2
    width = half // count_trans
    planes = row_pos.shape[0]
    bins = efficiency.shape[0]
    rows_out = length // (count_trans * count_los)
    plane_id = plane_of_slot[lax.axis_index("los")]
    even, odd = full_table(length, width)

    cols_hat = hat_rows(col_pos[plane_id], cells)
    sampled = dot(density[0], cols_hat, ((1,), (1,)))
    plus = (sampled[:, :half] + sampled[:, half:]).astype(BF)
    minus = (sampled[:, :half] - sampled[:, half:]).astype(BF)
    spec = jnp.concatenate([dot(plus, even, ((1,), (0,))), dot(minus, odd, ((1,), (0,)))], axis=1).astype(BF)
    columns = lax.all_to_all(spec, "trans", split_axis=1, concat_axis=0, tiled=True)

    rows_hat = hat_rows(row_pos[plane_id], cells)
    mapped = dot(rows_hat, columns, ((1,), (0,)))
    plus = (mapped[:half] + mapped[half:]).astype(BF)
    minus = (mapped[:half] - mapped[half:]).astype(BF)
    freq = jnp.concatenate([dot(even, plus, ((0,), (0,))), dot(odd, minus, ((0,), (0,)))], axis=0)
    wave_np, phase_np = slot_layout(length, width)
    nyq_np = wave_np == half
    k1 = jnp.asarray(np.where(nyq_np, -half, wave_np), F32)[:, None]
    row_nyq = jnp.asarray(nyq_np)[:, None]
    row_sign = jnp.asarray(np.where(phase_np > 0, 1.0, -1.0), F32)[:, None]
    k2, lane_nyq, lane_sine = lane_waves(length, width, lax.axis_index("trans"))
    lane_sign = jnp.where(lane_sine, 1.0, -1.0)
    square = jnp.maximum(k1 * k1 + k2 * k2, 1.0)
    scale1 = jnp.asarray(np.where((wave_np == 0) | nyq_np, 1.0, 2.0) / length, F32)[:, None]
    scale2 = jnp.where((k2 == 0.0) | lane_nyq, 1.0, 2.0) / length
    scale = scale1 * scale2 / square
    d1 = (k1 * k1 - k2 * k2) * scale
    d2 = 2.0 * k1 * k2 * scale
    grid = freq.reshape(-1, 2, width, 2 * width)
    swap_rows = jnp.flip(grid, 1).reshape(freq.shape)
    swap_lanes = jnp.roll(freq, width, axis=1)
    swap_both = jnp.roll(swap_rows, width, axis=1)
    first = d1 * freq
    first = first + jnp.where(lane_nyq & ~row_nyq, row_sign * d2 * swap_rows, 0.0)
    first = first + jnp.where(row_nyq & ~lane_nyq, lane_sign * d2 * swap_lanes, 0.0)
    second = jnp.where(
        row_nyq,
        jnp.where(lane_nyq, d2 * freq, 0.0),
        jnp.where(lane_nyq, 0.0, -row_sign * lane_sign * d2 * swap_both),
    )
    fields = jnp.concatenate([first, second], axis=1).astype(BF)
    part_e = dot(even, fields[:half], ((1,), (0,)))
    part_o = dot(odd, fields[half:], ((1,), (0,)))
    back = jnp.concatenate([part_e + part_o, part_e - part_o], axis=0).astype(BF)

    back = back.reshape(count_trans * count_los, rows_out, 2, 2 * width)
    arrived = lax.all_to_all(back, ("trans", "los"), split_axis=0, concat_axis=0, tiled=True)
    arrived = arrived.reshape(count_trans, count_los, rows_out, 2, 2 * width).transpose(1, 3, 2, 0, 4)
    arrived = arrived.reshape(count_los * 2 * rows_out, length)
    part_e = dot(arrived[:, :half], even, ((1,), (1,)))
    part_o = dot(arrived[:, half:], odd, ((1,), (1,)))
    maps = jnp.concatenate([part_e + part_o, part_e - part_o], axis=1)
    maps = maps.reshape(count_los, 2, rows_out, length)
    slot_eff = efficiency[:, plane_of_slot]
    behind = jnp.arange(bins)[:, None] >= plane_bin[plane_of_slot][None, :]
    weights = jnp.where(behind, slot_eff, 0.0)
    total = 0.0
    for slot in range(planes):
        total = total + weights[None, :, slot, None, None] * maps[slot][:, None]
    return total


def solution(mesh):
    placed = (P("los", "trans", None), P(), P(), P(), P(), P())
    return jax.shard_map(
        body_plain,
        mesh=mesh,
        in_specs=placed,
        out_specs=P(None, None, ("trans", "los"), None),
        check_vma=False,
    )
```

time: 634 us -> 93 us (0.15)
  local copies, waits for them, and re-layouts: 147 us -> 8.79 us
  matrix products: 145 us -> 15.3 us
  blocking collectives: 122 us -> 0 us
  waiting for transfers between devices: 115 us -> 39.8 us
  other arithmetic: 64.5 us -> 14.9 us
  between operations: 14.4 us -> 2.38 us
  starting transfers between devices: 19.9 us -> 11.3 us
    dot_general x37 -> x10, matrix products: 145 us -> 15.3 us  [dot(): return lax.dot_general(a, b, (dims, ((), ())), preferred_element_type=F32)]
    all_to_all x2 -> x0, blocking collectives: 122 us -> none  [the longest x1 114 us: body(): lax.all_to_all(returned, 'trans', split_axis=1, concat_axis=3, tiled=True)]
    all_to_all x3 -> x2, waiting for transfers between devices: 105 us -> 39.8 us  [the longest x1 24.9 us: body_plain(): lax.all_to_all(back, ('trans', 'los'), split_axis=0, concat_axis=0, tiled...]
    unnamed x54 -> x35, local copies, waits for them, and re-layouts: 33.2 us -> 1.58 us
    unnamed x2 -> x0, other arithmetic: 23.1 us -> none
    transpose x2 -> x1, local copies, waits for them, and re-layouts: 22.1 us -> 0.68 us  [body_plain(): arrived.reshape(count_trans, count_los, rows_out, 2, 2 * width)]
    all_to_all x8 -> x0, local copies, waits for them, and re-layouts: 21.2 us -> none  [the longest x3 14.6 us: body(): lax.all_to_all(returned, 'trans', split_axis=1, concat_axis=3, tiled=True)]
    mul x4 -> x1, local copies, waits for them, and re-layouts: 18.3 us -> 0.01 us  [body_plain(): total = total + weights[None, :, slot, None, None] * maps[slot][:, None]]
  transfers between devices with their start and end apart: 5 -> 2, of which waited for: 4 -> 2; matrix products, arithmetic and copies ran while one was open for 4% -> 1% of each run, Pallas kernels for 0% -> 0%
where the time goes in v1:
time: 93 us; the launch traced here: 92.5 us
  waiting for transfers between devices  39.8 us (43%)
  matrix products  15.3 us (16%)
  other arithmetic  14.9 us (16%)
  starting transfers between devices  11.3 us (12%)
  local copies, waits for them, and re-layouts  8.79 us (9%)
  between operations  2.38 us (3%)
    all_to_all x1, waiting for transfers between devices, body_plain(): lax.all_to_all(back, ('trans', 'los'), split_axis=0, concat_axis=0, tiled...  24.9 us
    dot_general x10, matrix products, dot(): return lax.dot_general(a, b, (dims, ((), ())), preferred_element_type=F32)  15.3 us
    all_to_all x1, waiting for transfers between devices, body_plain(): lax.all_to_all(spec, 'trans', split_axis=1, concat_axis=0, tiled=True)  15 us
    all_to_all x1, starting transfers between devices, body_plain(): lax.all_to_all(spec, 'trans', split_axis=1, concat_axis=0, tiled=True)  8.35 us
    another operation x2, other arithmetic  5.46 us
    all_to_all x1, starting transfers between devices, body_plain(): lax.all_to_all(back, ('trans', 'los'), split_axis=0, concat_axis=0, tiled...  2.93 us
    convert_element_type x1, other arithmetic, full_table(): table = table.reshape(half, 2 * half).astype(BF)  2.78 us
    concatenate x2, other arithmetic, body_plain(): jnp.concatenate([dot(even, plus, ((0,), (0,))), dot(odd, minus, ((0,), (0...  2.72 us
  transfers between devices with their start and end apart: 2, of which 2 were waited for; matrix products, arithmetic and copies ran while one was open for 1% of the time, Pallas kernels for 0%

profile of v1, /device:TPU:0, one launch (start us, length us, event | category | flops | bytes accessed | tf_op | source)
XLA Modules:
  0.0 92.5 jit_solution(424537392469630556)
XLA Ops:
  0.0 0.0 copy-start
  0.0 1.3 %dynamic_slice.9 = s32[1]{0:T(128)} dynamic-slice(s32[2]{0:T(128)} %param.17, s32[]{:T(128)S(6)} %select_n.149), dynamic_slice_sizes={1} | dynamic-slice | bytes 12 | tf_op jit(solution)/shard_map/dynamic_slice | solution.py:83
  3.2 0.8 constant_dynamic-slice_fusion
  4.0 2.8 %subtract_convert_fusion = bf16[32,32,2048]{2,1,0:T(8,128)(2,1)S(1)} fusion(f32[32,2048]{1,0:T(8,128)} %constant.91.clone, f32[32,2048]{1,0:T(8,128)} %constant.89.clone, f32[32,2048]{1,0:T(8,128)} %constant.90.clone, f32[32,2048]{1,0:T(8,128)} %constant.88.clone), kind=kLoop, calls=%fused_computation.8 | loop fusion | flops 8388608 | bytes 5242880 | tf_op jit(solution)/shard_map/convert_element_type | solution.py:43
  6.8 0.0 copy-start.2
  6.8 0.0 copy-done
  6.9 4.1 %fusion.2 = f32[128,2048]{0,1:T(8,128)S(1)} fusion(bf16[2048]{0:T(1024)(128)(2,1)S(1)} %get-tuple-element.26, s32[2048]{0:T(1024)S(1)} %get-tuple-element.24, bf16[2048]{0:T(1024)(128)(2,1)S(1)} %get-tuple-element.25, s32[2048]{0:T(1024)S(1)} %get-tuple-element.23, bf16[1,128,2048]{2,1,0:T(8,128)(2,1)S(1)} %copy-done), kind=kOutput, calls=%fused_computation.12 | convolution fusion | flops 1090519040 | bytes 1597440 | tf_op jit(solution)/shard_map/dot_general | solution.py:58
  10.9 0.5 fusion.28
  11.4 0.0 copy-done.2
  11.4 0.5 fusion.25
  12.0 0.8 pad_maximum_fusion.5
  12.8 8.3 %all-to-all-start = ((bf16[128,16,128]{2,0,1:T(8,128)(2,1)}), bf16[128,16,128]{2,0,1:T(8,128)(2,1)S(1)}, u32[]{:S(2)}, u32[]{:S(2)}) async-start(bf16[128,16,128]{2,0,1:T(8,128)(2,1)} %pad_maximum_fusion.5), calls=%async_computation | async-start | bytes 1048576 | tf_op jit(solution)/shard_map/all_to_all | solution.py:91
  21.3 15.0 %all-to-all-done = bf16[128,16,128]{2,0,1:T(8,128)(2,1)S(1)} async-done(((bf16[128,16,128]{2,0,1:T(8,128)(2,1)}), bf16[128,16,128]{2,0,1:T(8,128)(2,1)S(1)}, u32[]{:S(2)}, u32[]{:S(2)}) %all-to-all-start) | async-done | bytes 524320 | tf_op jit(solution)/shard_map/all_to_all | solution.py:91
  36.3 0.0 copy-start.3
  36.3 5.9 %fusion = f32[2048,128]{1,0:T(8,128)S(1)} fusion(bf16[2048,128]{1,0:T(8,128)(2,1)S(1)} %bitcast.60, bf16[2048]{0:T(1024)(128)(2,1)S(1)} %get-tuple-element.22, s32[2048]{0:T(1024)S(1)} %get-tuple-element.20, bf16[2048]{0:T(1024)(128)(2,1)S(1)} %get-tuple-element.21, s32[2048]{0:T(1024)S(1)} %get-tuple-element.19), kind=kOutput, calls=%fused_computation.9 | convolution fusion | flops 1090519040 | bytes 1597440 | tf_op jit(solution)/shard_map/dot_general | solution.py:58
  42.2 0.0 copy-done.3
  42.2 0.7 fusion.15
  42.9 0.7 fusion.7
  43.7 1.6 %fusion.31 = (f32[2048,64]{1,0:T(8,128)}, f32[2048,64]{1,0:T(8,128)}) fusion(f32[1024,128]{1,0:T(8,128)S(1)} %fusion.15, f32[1024,128]{1,0:T(8,128)S(1)} %fusion.7), kind=kLoop, calls=%fused_computation.40 | loop fusion | flops 262144 | bytes 2097152 | tf_op jit(solution)/shard_map/concatenate | solution.py:97
  45.3 0.0 copy-start.9
  45.3 0.0 copy-start.14
  45.3 1.1 %pad_maximum_fusion = f32[2048,128]{1,0:T(8,128)} fusion(f32[1024,128]{1,0:T(8,128)S(1)} %fusion.7, f32[1024,128]{1,0:T(8,128)S(1)} %fusion.15), kind=kLoop, calls=%fused_computation.17 | loop fusion | flops 262144 | bytes 2097152 | tf_op jit(solution)/shard_map/concatenate | solution.py:97
  46.4 1.3 %rev.4 = f32[16,2,64,128]{3,2,1,0:T(8,128)S(1)} reverse(f32[16,2,64,128]{3,2,1,0:T(8,128)} %bitcast.53), dimensions={1} | reverse | bytes 2097152 | tf_op jit(solution)/shard_map/jit(_flip)/rev | solution.py:112
  47.7 0.0 copy-start.6
  47.7 0.0 copy-start.7
  47.7 0.0 copy-start.12
  47.7 0.0 copy-start.15
  47.7 0.3 fusion.60
  48.1 0.0 copy-done.9
  48.1 0.0 copy-done.10
  48.1 0.0 copy-done.11
  48.1 0.0 copy-done.13
  48.1 0.0 copy-done.14
  48.1 0.0 copy-start.4
  48.1 2.6 %fusion.39 = bf16[2048,128]{1,0:T(8,128)(2,1)S(1)} fusion(f32[2048,64]{1,0:T(8,128)S(1)} %get-tuple-element.16, f32[2048,64]{1,0:T(8,128)S(1)} %get-tuple-element.15, f32[2048]{0:T(1024)S(1)} %copy-done.13, f32[128]{0:T(128)S(1)} %get-tuple-element.32, f32[128]{0:T(128)S(1)} %get-tuple-element.8, f32[2048]{0:T(1024)S(1)} %copy-done.11, ...), kind=kLoop, calls=%fused_computation.52 | loop fusion | flops 4194304 | bytes 2658432 | tf_op jit(solution)/shard_map/convert.3
  50.7 0.0 copy-done.6
  50.7 0.0 copy-done.7
  50.7 0.0 copy-done.12
  50.7 0.0 copy-done.15
  50.7 2.9 %fusion.36 = bf16[2048,128]{1,0:T(8,128)(2,1)S(1)} fusion(f32[2048,64]{1,0:T(8,128)S(1)} %copy-done.7, f32[2048,64]{1,0:T(8,128)S(1)} %copy-done.6, f32[128]{0:T(128)S(1)} %get-tuple-element.32, f32[128]{0:T(128)S(1)} %get-tuple-element.8, f32[2048]{0:T(1024)S(1)} %copy-done.11, f32[2048]{0:T(1024)S(1)} %copy-done.12, f32[128]{0:T(128)S(1)} %get-tuple-element.33, ...), kind=kLoop, calls=%fused_computation.48 | loop fusion | flops 5767168 | bytes 3709184 | tf_op jit(solution)/shard_map/convert.2
  53.7 0.0 copy-done.4
  53.7 0.7 fusion.5
  54.4 0.7 add_convert_fusion
  55.1 0.0 copy-start.16
  55.1 0.0 copy-start.8
  55.1 0.0 copy-start.1
  55.1 0.1 pad_maximum_fusion.2
  55.2 0.3 convert_element_type.81
  55.5 1.3 %copy.19 = bf16[32,64,2,128]{3,1,2,0:T(8,128)(2,1)} copy(bf16[32,64,2,128]{3,2,1,0:T(2,128)(2,1)S(1)} %convert_element_type.81) | data formatting | bytes 2097152 | tf_op jit(solution)/shard_map/convert_element_type | solution.py:126
  56.8 2.9 %all-to-all-start.1 = ((bf16[32,64,2,128]{3,1,2,0:T(8,128)(2,1)}), bf16[32,64,2,128]{3,1,2,0:T(8,128)(2,1)S(1)}, u32[]{:S(2)}, u32[]{:S(2)}) async-start(bf16[32,64,2,128]{3,1,2,0:T(8,128)(2,1)} %copy.19), calls=%async_computation.1 | async-start | bytes 2097152 | tf_op jit(solution)/shard_map/all_to_all | solution.py:129
  59.7 0.0 copy-done.16
  59.8 0.0 copy-done.8
  59.8 0.6 gather_fusion.1
  60.3 0.0 copy-done.1
  60.3 0.6 gather_fusion
  61.0 0.1 compare_select_fusion.1
  61.1 24.9 %all-to-all-done.1 = bf16[32,64,2,128]{3,1,2,0:T(8,128)(2,1)S(1)} async-done(((bf16[32,64,2,128]{3,1,2,0:T(8,128)(2,1)}), bf16[32,64,2,128]{3,1,2,0:T(8,128)(2,1)S(1)}, u32[]{:S(2)}, u32[]{:S(2)}) %all-to-all-start.1) | async-done | bytes 1048608 | tf_op jit(solution)/shard_map/all_to_all | solution.py:129
  85.9 0.7 copy.20
  86.6 0.3 copy.27
  86.9 1.2 %copy-done.5 = bf16[32,32,2048]{2,1,0:T(8,128)(2,1)S(1)} copy-done((bf16[32,32,2048]{2,1,0:T(8,128)(2,1)S(1)}, bf16[32,32,2048]{2,1,0:T(8,128)(2,1)}, u32[]{:S(2)}) %copy-start.5) | copy-done | bytes 4194328
  88.1 0.7 fusion.3
  88.9 0.8 fusion.59
  89.6 0.2 fusion.33
  89.9 2.7 %multiply_add_fusion = f32[2,4,64,2048]{3,2,1,0:T(8,128)} fusion(f32[2,64,2048]{2,1,0:T(8,128)S(1)} %bitcast.55, f32[4]{0:T(128)S(1)} %get-tuple-element.28, f32[2,64,2048]{2,1,0:T(8,128)S(1)} %bitcast.54, f32[4]{0:T(128)S(1)} %get-tuple-element.27), kind=kLoop, calls=%fused_computation.11 | loop fusion | flops 3145728 | bytes 6291488 | tf_op jit(solution)/shard_map/add | solution.py:141
  (16 shorter events, 0.2 us)
Async XLA Ops:
  0.0 6.8 %copy-start = (bf16[1,128,2048]{2,1,0:T(8,128)(2,1)S(1)}, bf16[1,128,2048]{2,1,0:T(8,128)(2,1)}, u32[]{:S(2)}) copy-start(bf16[1,128,2048]{2,1,0:T(8,128)(2,1)} %param.14) | copy-start | bytes 1572868
  6.8 4.6 %copy-start.2 = (bf16[32,32,2048]{2,1,0:T(8,128)(2,1)}, bf16[32,32,2048]{2,1,0:T(8,128)(2,1)S(1)}, u32[]{:S(2)}) copy-start(bf16[32,32,2048]{2,1,0:T(8,128)(2,1)S(1)} %subtract_convert_fusion) | copy-start | bytes 12582916
  12.8 23.4 %all-to-all-start = ((bf16[128,16,128]{2,0,1:T(8,128)(2,1)}), bf16[128,16,128]{2,0,1:T(8,128)(2,1)S(1)}, u32[]{:S(2)}, u32[]{:S(2)}) async-start(bf16[128,16,128]{2,0,1:T(8,128)(2,1)} %pad_maximum_fusion.5), calls=%async_computation | async-start | bytes 1048576 | tf_op jit(solution)/shard_map/all_to_all | solution.py:91
  36.3 5.9 %copy-start.3 = (bf16[32,32,2048]{2,1,0:T(8,128)(2,1)S(1)}, bf16[32,32,2048]{2,1,0:T(8,128)(2,1)}, u32[]{:S(2)}) copy-start(bf16[32,32,2048]{2,1,0:T(8,128)(2,1)} %copy-done.2) | copy-start | bytes 12582916
  45.3 2.8 %copy-start.9 = (f32[2048]{0:T(1024)S(1)}, f32[2048]{0:T(1024)}, u32[]{:S(2)}) copy-start(f32[2048]{0:T(1024)} %constant.95.clone) | copy-start | bytes 24580
  45.3 2.8 %copy-start.10 = (f32[2048]{0:T(1024)S(1)}, f32[2048]{0:T(1024)}, u32[]{:S(2)}) copy-start(f32[2048]{0:T(1024)} %constant.97) | copy-start | bytes 24580
  45.3 2.8 %copy-start.11 = (f32[2048]{0:T(1024)S(1)}, f32[2048]{0:T(1024)}, u32[]{:S(2)}) copy-start(f32[2048]{0:T(1024)} %constant.99) | copy-start | bytes 24580
  45.3 2.8 %copy-start.13 = (f32[2048]{0:T(1024)S(1)}, f32[2048]{0:T(1024)}, u32[]{:S(2)}) copy-start(f32[2048]{0:T(1024)} %constant.100) | copy-start | bytes 24580
  45.3 2.8 %copy-start.14 = (pred[2048]{0:T(1024)(128)(4,1)S(1)}, pred[2048]{0:T(1024)(128)(4,1)}, u32[]{:S(2)}) copy-start(pred[2048]{0:T(1024)(128)(4,1)} %constant.93.clone) | copy-start | bytes 6148
  47.7 3.0 %copy-start.6 = (f32[2048,64]{1,0:T(8,128)S(1)}, f32[2048,64]{1,0:T(8,128)}, u32[]{:S(2)}) copy-start(f32[2048,64]{1,0:T(8,128)} %get-tuple-element.17) | copy-start | bytes 1572868
  47.7 3.0 %copy-start.7 = (f32[2048,64]{1,0:T(8,128)S(1)}, f32[2048,64]{1,0:T(8,128)}, u32[]{:S(2)}) copy-start(f32[2048,64]{1,0:T(8,128)} %get-tuple-element.18) | copy-start | bytes 1572868
  47.7 3.0 %copy-start.12 = (f32[2048]{0:T(1024)S(1)}, f32[2048]{0:T(1024)}, u32[]{:S(2)}) copy-start(f32[2048]{0:T(1024)} %constant.94.clone) | copy-start | bytes 24580
  47.7 3.0 %copy-start.15 = (pred[2048]{0:T(1024)(128)(4,1)S(1)}, pred[2048]{0:T(1024)(128)(4,1)}, u32[]{:S(2)}) copy-start(pred[2048]{0:T(1024)(128)(4,1)} %constant.98) | copy-start | bytes 6148
  48.1 5.5 %copy-start.4 = (bf16[32,32,2048]{2,1,0:T(8,128)(2,1)S(1)}, bf16[32,32,2048]{2,1,0:T(8,128)(2,1)}, u32[]{:S(2)}) copy-start(bf16[32,32,2048]{2,1,0:T(8,128)(2,1)} %copy-done.2) | copy-start | bytes 12582916
  55.1 4.6 %copy-start.16 = (s32[2]{0:T(128)S(1)}, s32[2]{0:T(128)}, u32[]{:S(2)}) copy-start(s32[2]{0:T(128)} %param.17) | copy-start | bytes 28
  55.1 4.6 %copy-start.8 = (f32[4,2]{0,1:T(2,128)S(1)}, f32[4,2]{0,1:T(2,128)}, u32[]{:S(2)}) copy-start(f32[4,2]{0,1:T(2,128)} %param.19) | copy-start | bytes 100
  55.1 5.2 %copy-start.1 = (s32[2]{0:T(128)S(1)}, s32[2]{0:T(128)}, u32[]{:S(2)}) copy-start(s32[2]{0:T(128)} %param.18) | copy-start | bytes 28
  56.8 29.1 %all-to-all-start.1 = ((bf16[32,64,2,128]{3,1,2,0:T(8,128)(2,1)}), bf16[32,64,2,128]{3,1,2,0:T(8,128)(2,1)S(1)}, u32[]{:S(2)}, u32[]{:S(2)}) async-start(bf16[32,64,2,128]{3,1,2,0:T(8,128)(2,1)} %copy.19), calls=%async_computation.1 | async-start | bytes 2097152 | tf_op jit(solution)/shard_map/all_to_all | solution.py:129
  85.9 2.2 %copy-start.5 = (bf16[32,32,2048]{2,1,0:T(8,128)(2,1)S(1)}, bf16[32,32,2048]{2,1,0:T(8,128)(2,1)}, u32[]{:S(2)}) copy-start(bf16[32,32,2048]{2,1,0:T(8,128)(2,1)} %copy-done.2) | copy-start | bytes 12582916

commit v2 on v1

--- a/solution.py
+++ b/solution.py
@@ -1,9 +1,11 @@
-import math
+import functools
 
 import jax
 import jax.numpy as jnp
 import numpy as np
 from jax import lax
+from jax.experimental import pallas as pl
+from jax.experimental.pallas import tpu as pltpu
 from jax.sharding import PartitionSpec as P
 
 BF = jnp.bfloat16
@@ -142,10 +144,299 @@
     return total
 
 
+def fold_waves(length, width, block, inner):
+    blocks = length // 2 // width
+    is_sine = inner >= width
+    member = jnp.where(is_sine, inner - width, inner)
+    odd = (block >= blocks // 2).astype(jnp.int32)
+    wave = 2 * ((block - odd * (blocks // 2)) * width + member) + odd
+    nyquist = is_sine & (wave == 0)
+    ends = (wave == 0) & ((block == 0) | ~is_sine)
+    wave = jnp.where(nyquist, -(length // 2), wave)
+    return wave.astype(F32), nyquist, is_sine, ends
+
+
+def fill_hat(out_ref, low_ref, frac_ref, positions_on_lanes):
+    cells = out_ref.shape[0]
+    part = 128
+
+    def step(i, carry):
+        rows = pl.ds(pl.multiple_of(i * part, part), part)
+        shape = (part, out_ref.shape[1])
+        if positions_on_lanes:
+            low, frac = low_ref[...], frac_ref[...]
+            index = lax.broadcasted_iota(jnp.int32, shape, 0) + i * part
+        else:
+            low, frac = low_ref[rows, :], frac_ref[rows, :]
+            index = lax.broadcasted_iota(jnp.int32, shape, 1)
+        high = jnp.where(low == cells - 1, 0, low + 1)
+        value = jnp.where(index == high, frac, 0.0)
+        value = jnp.where(index == low, 1.0 - frac, value)
+        out_ref[rows, :] = value.astype(BF)
+        return carry
+
+    lax.fori_loop(0, cells // part, step, 0)
+
+
+def middle_kernel(
+    count_trans, count_los, length,
+    dens_ref, clow_ref, cfrac_ref, rlow_ref, rfrac_ref, cos_a, sin_a, cos_b, sin_b,
+    out_ref, table_out,
+    table, hat, halves, send1, recv1, turned, fields, send2,
+    ssem1, rsem1, ssem2, rsem2, lsem,
+):
+    me_t = lax.axis_index("trans")
+    me_l = lax.axis_index("los")
+    devices = count_trans * count_los
+    me = me_t * count_los + me_l
+    half = length // 2
+    width = half // count_trans
+    lanes = 2 * width
+    rows_out = length // devices
+    chunk = 256
+    barrier = pltpu.get_barrier_semaphore()
+
+    def greet(i, carry):
+        other = lax.rem(me + i, devices)
+        pl.semaphore_signal(
+            barrier, inc=1,
+            device_id=(other // count_los, lax.rem(other, count_los)),
+            device_id_type=pl.DeviceIdType.MESH,
+        )
+        return carry
+
+    lax.fori_loop(1, devices, greet, 0)
+
+    def table_step(i, carry):
+        rows = pl.ds(pl.multiple_of(i * STEP, STEP), STEP)
+        value = cos_a[pl.ds(i, 1), :] * cos_b[...] - sin_a[pl.ds(i, 1), :] * sin_b[...]
+        table[rows, :] = value.astype(BF)
+        return carry
+
+    lax.fori_loop(0, half // STEP, table_step, 0)
+    table_copy = pltpu.make_async_copy(table, table_out, lsem.at[0])
+    table_copy.start()
+
+    fill_hat(hat, clow_ref, cfrac_ref, True)
+    for c in range(half // chunk):
+        low = jnp.dot(dens_ref[...], hat[:, c * chunk : (c + 1) * chunk], preferred_element_type=F32)
+        high = jnp.dot(
+            dens_ref[...], hat[:, half + c * chunk : half + (c + 1) * chunk],
+            preferred_element_type=F32,
+        )
+        halves[0, :, c * chunk : (c + 1) * chunk] = (low + high).astype(BF)
+        halves[1, :, c * chunk : (c + 1) * chunk] = (low - high).astype(BF)
+    for c in range(length // chunk):
+        spec = jnp.dot(
+            halves[c * chunk // half], table[:, c * chunk : (c + 1) * chunk],
+            preferred_element_type=F32,
+        ).astype(BF)
+        for k in range(chunk // lanes):
+            send1[c * (chunk // lanes) + k] = spec[:, k * lanes : (k + 1) * lanes]
+
+    pl.semaphore_wait(barrier, devices - 1)
+
+    def copy1(target, source):
+        return pltpu.make_async_remote_copy(
+            src_ref=send1.at[target], dst_ref=recv1.at[source],
+            send_sem=ssem1.at[target], recv_sem=rsem1.at[source],
+            device_id=(target, me_l), device_id_type=pl.DeviceIdType.MESH,
+        )
+
+    def start1(i, carry):
+        copy1(lax.rem(me_t + i, count_trans), me_t).start()
+        return carry
+
+    lax.fori_loop(1, count_trans, start1, 0)
+    own1 = pltpu.make_async_copy(send1.at[me_t], recv1.at[me_t], lsem.at[1])
+    own1.start()
+    fill_hat(hat, rlow_ref, rfrac_ref, False)
+    own1.wait()
+
+    def wait1(i, carry):
+        other = lax.rem(me_t + i, count_trans)
+        copy1(other, me_t).wait_send()
+        copy1(me_t, other).wait_recv()
+        return carry
+
+    lax.fori_loop(1, count_trans, wait1, 0)
+
+    columns = recv1[...].reshape(hat.shape[1], lanes)
+    for c in range(half // chunk):
+        low = jnp.dot(hat[c * chunk : (c + 1) * chunk, :], columns, preferred_element_type=F32)
+        high = jnp.dot(
+            hat[half + c * chunk : half + (c + 1) * chunk, :], columns,
+            preferred_element_type=F32,
+        )
+        turned[0, :, c * chunk : (c + 1) * chunk] = (low + high).T.astype(BF)
+        turned[1, :, c * chunk : (c + 1) * chunk] = (low - high).T.astype(BF)
+
+    shape = (lanes, lanes)
+    k2, lane_nyq, lane_sine, lane_end = fold_waves(
+        length, width, me_t, lax.broadcasted_iota(jnp.int32, shape, 0)
+    )
+    lane_sign = jnp.where(lane_sine, 1.0, -1.0)
+    scale2 = jnp.where(lane_end | lane_nyq, 1.0, 2.0) * (1.0 / length)
+    inner = lax.broadcasted_iota(jnp.int32, shape, 1)
+    for c in range(length // chunk):
+        freq2 = jnp.dot(
+            turned[c * chunk // half], table[:, c * chunk : (c + 1) * chunk],
+            preferred_element_type=F32,
+        )
+        for k in range(chunk // lanes):
+            block = c * (chunk // lanes) + k
+            freq = freq2[:, k * lanes : (k + 1) * lanes]
+            k1, row_nyq, row_sine, row_end = fold_waves(length, width, jnp.int32(block), inner)
+            row_sign = jnp.where(row_sine, 1.0, -1.0)
+            scale1 = jnp.where(row_end | row_nyq, 1.0, 2.0) * (1.0 / length)
+            scale = scale1 * scale2 / jnp.maximum(k1 * k1 + k2 * k2, 1.0)
+            d1 = (k1 * k1 - k2 * k2) * scale
+            d2 = 2.0 * k1 * k2 * scale
+            swap_rows = pltpu.roll(freq, width, 1)
+            swap_lanes = jnp.concatenate([freq[width:], freq[:width]], axis=0)
+            swap_both = pltpu.roll(swap_lanes, width, 1)
+            first = d1 * freq
+            extra = jnp.where(lane_nyq, row_sign * d2 * swap_rows, 0.0)
+            second = jnp.where(lane_nyq, 0.0, -row_sign * lane_sign * d2 * swap_both)
+            if block == 0:
+                extra = jnp.where(
+                    row_nyq, jnp.where(lane_nyq, 0.0, lane_sign * d2 * swap_lanes), extra
+                )
+                second = jnp.where(row_nyq, jnp.where(lane_nyq, d2 * freq, 0.0), second)
+            where = slice(block * lanes, (block + 1) * lanes)
+            fields[:lanes, where] = (first + extra).astype(BF)
+            fields[lanes:, where] = second.astype(BF)
+
+    contract = (((1,), (1,)), ((), ()))
+    per = chunk // rows_out
+    for c in range(half // chunk):
+        rows = slice(c * chunk, (c + 1) * chunk)
+        part_e = lax.dot_general(
+            table[rows, :half], fields[:, :half], contract, preferred_element_type=F32
+        )
+        part_o = lax.dot_general(
+            table[rows, half:], fields[:, half:], contract, preferred_element_type=F32
+        )
+        for offset, value in ((0, part_e + part_o), (devices // 2, part_e - part_o)):
+            value = value.astype(BF)
+            for k in range(per):
+                for comp in range(2):
+                    send2[offset + c * per + k, comp] = value[
+                        k * rows_out : (k + 1) * rows_out, comp * lanes : (comp + 1) * lanes
+                    ]
+
+    def place(other):
+        begin = pl.multiple_of((other // count_los) * lanes, lanes)
+        return out_ref.at[lax.rem(other, count_los), :, :, pl.ds(begin, lanes)]
+
+    def copy2(target, source):
+        return pltpu.make_async_remote_copy(
+            src_ref=send2.at[target], dst_ref=place(source),
+            send_sem=ssem2.at[target], recv_sem=rsem2.at[source],
+            device_id=(target // count_los, lax.rem(target, count_los)),
+            device_id_type=pl.DeviceIdType.MESH,
+        )
+
+    def start2(i, carry):
+        copy2(lax.rem(me + i, devices), me).start()
+        return carry
+
+    lax.fori_loop(1, devices, start2, 0)
+    own2 = pltpu.make_async_copy(send2.at[me], place(me), lsem.at[2])
+    own2.start()
+    own2.wait()
+
+    def wait2(i, carry):
+        other = lax.rem(me + i, devices)
+        copy2(other, me).wait_send()
+        copy2(me, other).wait_recv()
+        return carry
+
+    lax.fori_loop(1, devices, wait2, 0)
+    table_copy.wait()
+
+
+def body_kernel(density, row_pos, col_pos, plane_of_slot, plane_bin, efficiency):
+    count_trans = lax.axis_size("trans")
+    count_los = lax.axis_size("los")
+    rows_in, cells = density.shape[1:]
+    length = row_pos.shape[1]
+    half = length // 2
+    width = half // count_trans
+    lanes = 2 * width
+    planes = row_pos.shape[0]
+    bins = efficiency.shape[0]
+    devices = count_trans * count_los
+    rows_out = length // devices
+
+    slots = jnp.arange(planes, dtype=jnp.int32)
+    plane_id = jnp.sum(jnp.where(slots == lax.axis_index("los"), plane_of_slot, 0))
+
+    def split(positions):
+        here = jnp.sum(jnp.where((slots == plane_id)[:, None], positions, 0.0), axis=0)
+        base = jnp.floor(here)
+        low = base.astype(jnp.int32)
+        return jnp.where(low >= cells, low - cells, low), here - base
+
+    clow, cfrac = split(col_pos)
+    rlow, rfrac = split(row_pos)
+    tables = [jnp.asarray(t) for t in small_tables(length, width)]
+    vmem = pl.BlockSpec(memory_space=pltpu.VMEM)
+    arrived, table = pl.pallas_call(
+        functools.partial(middle_kernel, count_trans, count_los, length),
+        out_shape=[
+            jax.ShapeDtypeStruct((count_los, 2, rows_out, length), BF),
+            jax.ShapeDtypeStruct((half, length), BF),
+        ],
+        in_specs=[vmem] * 9,
+        out_specs=[vmem, pl.BlockSpec(memory_space=pl.ANY)],
+        scratch_shapes=[
+            pltpu.VMEM((half, length), BF),
+            pltpu.VMEM((length, cells), BF),
+            pltpu.VMEM((2, rows_in, half), BF),
+            pltpu.VMEM((count_trans, rows_in, lanes), BF),
+            pltpu.VMEM((count_trans, rows_in, lanes), BF),
+            pltpu.VMEM((2, lanes, half), BF),
+            pltpu.VMEM((2 * lanes, length), BF),
+            pltpu.VMEM((devices, 2, rows_out, lanes), BF),
+            pltpu.SemaphoreType.DMA((count_trans,)),
+            pltpu.SemaphoreType.DMA((count_trans,)),
+            pltpu.SemaphoreType.DMA((devices,)),
+            pltpu.SemaphoreType.DMA((devices,)),
+            pltpu.SemaphoreType.DMA((3,)),
+        ],
+        compiler_params=pltpu.CompilerParams(
+            collective_id=0, has_side_effects=True, vmem_limit_bytes=56 * 1024 * 1024
+        ),
+    )(
+        density[0], clow[None, :], cfrac[None, :], rlow[:, None], rfrac[:, None], *tables
+    )
+    arrived = arrived.reshape(count_los * 2 * rows_out, length)
+    part_e = dot(arrived[:, :half], table[:, :half], ((1,), (1,)))
+    part_o = dot(arrived[:, half:], table[:, half:], ((1,), (1,)))
+    maps = jnp.concatenate([part_e + part_o, part_e - part_o], axis=1)
+    maps = maps.reshape(count_los, 2, rows_out, length)
+    total = 0.0
+    for slot in range(planes):
+        chosen = slots == plane_of_slot[slot]
+        slot_eff = jnp.sum(jnp.where(chosen[None, :], efficiency, 0.0), axis=1)
+        first_bin = jnp.sum(jnp.where(chosen, plane_bin, 0))
+        weight = jnp.where(jnp.arange(bins) >= first_bin, slot_eff, 0.0)
+        total = total + weight[None, :, None, None] * maps[slot][:, None]
+    return total
+
+
+def body(density, row_pos, *rest):
+    length = row_pos.shape[1]
+    fits = length // lax.axis_size("trans") == 128 and density.shape[1] == 128
+    fits = fits and length % 512 == 0 and density.shape[2] == length
+    return (body_kernel if fits else body_plain)(density, row_pos, *rest)
+
+
 def solution(mesh):
     placed = (P("los", "trans", None), P(), P(), P(), P(), P())
     return jax.shard_map(
-        body_plain,
+        body,
         mesh=mesh,
         in_specs=placed,
         out_specs=P(None, None, ("trans", "los"), None),

time: 93 us -> 71.9 us (0.77)
  the two profiles are of different devices: /device:TPU:0 before, /device:TPU:15 now
where the time goes in v2:
time: 71.9 us; the launch traced here: 71.5 us
  Pallas kernels  51.6 us (72%)
  other arithmetic  13.7 us (19%)
  matrix products  4.48 us (6%)
  local copies, waits for them, and re-layouts  1.66 us (2%)
    pallas_call x1, Pallas kernels, body_kernel(): pl.pallas_call(functools.partial(middle_kernel, count_trans, count_los, l...  51.6 us
    dot_general x2, matrix products, dot(): return lax.dot_general(a, b, (dims, ((), ())), preferred_element_type=F32)  4.48 us
    add x1, other arithmetic, body_kernel(): total = total + weight[None, :, None, None] * maps[slot][:, None]  2.67 us
    reduce_sum x1, other arithmetic, body_kernel(): first_bin = jnp.sum(jnp.where(chosen, plane_bin, 0))  2 us
    select_n x2, other arithmetic, split(): return (jnp.where(low >= cells, low - cells, low), here - base)  1.75 us
    sub x2, other arithmetic, split(): return (jnp.where(low >= cells, low - cells, low), here - base)  1.68 us

profile of v2, /device:TPU:15, one launch (start us, length us, event | category | flops | bytes accessed | tf_op | source)
XLA Modules:
  0.0 71.5 jit_solution(4581266960852596425)
XLA Ops:
  0.0 1.3 %fusion.7 = s32[]{:T(128)} fusion(s32[2]{0:T(128)} %param.13, s32[]{:T(128)S(6)} %axis_index.12), kind=kLoop, calls=%fused_computation.22 | loop fusion | flops 5 | bytes 16 | tf_op jit(solution)/shard_map/reduce_sum | solution.py:373
  1.3 0.6 iota_compare_fusion.1
  1.9 0.8 %select_reduce_fusion = (f32[2048]{0:T(1024)S(1)}, f32[2048]{0:T(1024)S(1)}) fusion(f32[2,2048]{1,0:T(2,128)} %param.11, pred[2]{0:T(512)(128)(4,1)S(1)} %iota_compare_fusion.1, f32[2,2048]{1,0:T(2,128)} %param.12), kind=kLoop, calls=%fused_computation.13 | loop fusion | flops 12288 | bytes 49154 | tf_op jit(solution)/shard_map/reduce_sum | solution.py:376
  2.8 0.4 copy.13
  3.2 0.4 copy.14
  3.6 1.1 %sub.32.rfrac_ref = f32[2048,1]{1,0:T(8,128)} subtract(f32[2048,1]{1,0:T(8,128)S(1)} %copy.14, f32[2048,1]{1,0:T(8,128)S(1)} %copy.13) | non-fusion elementwise | flops 2048 | bytes 24576 | tf_op jit(solution)/shard_map/sub | solution.py:379
  4.7 1.1 %compare_select_fusion.rlow_ref = s32[2048,1]{1,0:T(8,128)} fusion(f32[2048,1]{1,0:T(8,128)S(1)} %copy.13), kind=kLoop, calls=%fused_computation.1 | loop fusion | flops 8192 | bytes 16384 | tf_op jit(solution)/shard_map/jit(_where)/select_n | solution.py:379
  5.8 0.6 compare_select_fusion.1.clow_ref
  6.4 0.6 floor_subtract_fusion.cfrac_ref
  7.0 51.6 %shard_map.100 = (bf16[2,2,64,2048]{3,2,1,0:T(8,128)(2,1)}, bf16[1024,2048]{1,0:T(8,128)(2,1)}) custom-call(bf16[128,2048]{1,0:T(8,128)(2,1)} %bitcast.10, s32[1,2048]{1,0:T(1,128)} %compare_select_fusion.1.clow_ref, f32[1,2048]{1,0:T(1,128)} %floor_subtract_fusion.cfrac_ref, s32[2048,1]{1,0:T(8,128)} %compare_select_fusion.rlow_ref, ...), custom_call_target="tpu_custom_call" | custom-call | tf_op jit(solution)/shard_map/pallas_call | solution.py:385
  58.6 0.0 copy-start
  58.6 2.6 %fusion = f32[256,1024]{1,0:T(8,128)S(1)} fusion(bf16[1024,2048]{1,0:T(8,128)(2,1)} %get-tuple-element.8, bf16[256,2048]{1,0:T(8,128)(2,1)} %bitcast.11), kind=kOutput, calls=%fused_computation.4 | convolution fusion | flops 536870912 | bytes 3670016 | tf_op jit(solution)/shard_map/dot_general | solution.py:60
  61.3 0.3 copy-done
  61.6 0.0 copy-start.1
  61.6 0.0 copy-start.2
  61.6 0.0 copy-start.3
  61.6 1.8 %fusion.8 = (f32[256,1024]{1,0:T(8,128)S(1)}, f32[256,1024]{1,0:T(8,128)S(1)}) fusion(f32[256,1024]{1,0:T(8,128)S(1)} %fusion, bf16[1024,2048]{1,0:T(8,128)(2,1)S(1)} %copy-done, bf16[256,2048]{1,0:T(8,128)(2,1)} %bitcast.12), kind=kOutput, calls=%fused_computation.28 | convolution fusion | flops 537395200 | bytes 5767168 | tf_op jit(solution)/shard_map/dot_general | solution.py:60
  63.5 0.1 fusion.4
  63.6 0.0 copy-done.1
  63.6 0.6 fusion.9
  64.2 0.6 iota_compare_fusion
  64.9 0.7 iota_compare_fusion.2
  65.6 0.0 copy-done.2
  65.6 0.1 select_reduce_fusion.3
  65.7 0.0 copy-done.3
  65.7 2.0 %select_reduce_fusion.5 = (s32[]{:T(128)}, s32[]{:T(128)}) fusion(s32[2]{0:T(128)S(1)} %copy-done.3, s32[]{:T(128)} %bitcast, s32[]{:T(128)} %bitcast.6), kind=kLoop, calls=%fused_computation.26 | loop fusion | flops 10 | bytes 24 | tf_op jit(solution)/shard_map/reduce_sum | solution.py:423
  67.7 1.2 %compare_select_fusion.2 = (f32[4]{0:T(128)S(1)}, f32[4]{0:T(128)S(1)}) fusion(f32[4]{0:T(128)S(1)} %get-tuple-element.10, s32[]{:T(128)} %get-tuple-element.12, f32[4]{0:T(128)S(1)} %get-tuple-element.9, s32[]{:T(128)} %get-tuple-element.11), kind=kLoop, calls=%fused_computation.17 | loop fusion | flops 16 | bytes 72 | tf_op jit(solution)/shard_map/jit(_where)/select_n | solution.py:424
  68.9 2.7 %multiply_add_fusion = f32[2,4,64,2048]{3,2,1,0:T(8,128)} fusion(f32[2,64,2048]{2,1,0:T(8,128)S(1)} %bitcast.9, f32[4]{0:T(128)S(1)} %get-tuple-element.22, f32[2,64,2048]{2,1,0:T(8,128)S(1)} %bitcast.8, f32[4]{0:T(128)S(1)} %get-tuple-element.23), kind=kLoop, calls=%fused_computation | loop fusion | flops 3145728 | bytes 6291488 | tf_op jit(solution)/shard_map/add | solution.py:425
  (1 shorter events, 0.0 us)
Async XLA Ops:
  58.6 3.0 %copy-start = (bf16[1024,2048]{1,0:T(8,128)(2,1)S(1)}, bf16[1024,2048]{1,0:T(8,128)(2,1)}, u32[]{:S(2)}) copy-start(bf16[1024,2048]{1,0:T(8,128)(2,1)} %get-tuple-element.8) | copy-start | bytes 12582916
  61.6 2.0 %copy-start.1 = (s32[2]{0:T(128)S(1)}, s32[2]{0:T(128)}, u32[]{:S(2)}) copy-start(s32[2]{0:T(128)} %param.13) | copy-start | bytes 28
  61.6 4.0 %copy-start.2 = (f32[4,2]{0,1:T(2,128)S(1)}, f32[4,2]{0,1:T(2,128)}, u32[]{:S(2)}) copy-start(f32[4,2]{0,1:T(2,128)} %param.15) | copy-start | bytes 100
  61.6 4.1 %copy-start.3 = (s32[2]{0:T(128)S(1)}, s32[2]{0:T(128)}, u32[]{:S(2)}) copy-start(s32[2]{0:T(128)} %param.14) | copy-start | bytes 28

commit v3 on v2

--- a/solution.py
+++ b/solution.py
@@ -156,23 +156,40 @@
     return wave.astype(F32), nyquist, is_sine, ends
 
 
-def fill_hat(out_ref, low_ref, frac_ref, positions_on_lanes):
+def split_positions(spot, pos_ref, plane_id, cells):
+    here = pos_ref[0:1, :]
+    for plane in range(1, pos_ref.shape[0]):
+        here = jnp.where(plane_id == plane, pos_ref[plane : plane + 1, :], here)
+    base = jnp.floor(here)
+    low = jnp.where(base >= cells, base - cells, base)
+    spot[0:1, :] = low
+    spot[1:2, :] = jnp.where(low == cells - 1, 0.0, low + 1.0)
+    spot[2:3, :] = here - base
+
+
+def fill_hat(out_ref, spot, positions_on_lanes):
     cells = out_ref.shape[0]
     part = 128
 
     def step(i, carry):
         rows = pl.ds(pl.multiple_of(i * part, part), part)
-        shape = (part, out_ref.shape[1])
-        if positions_on_lanes:
-            low, frac = low_ref[...], frac_ref[...]
-            index = lax.broadcasted_iota(jnp.int32, shape, 0) + i * part
-        else:
-            low, frac = low_ref[rows, :], frac_ref[rows, :]
-            index = lax.broadcasted_iota(jnp.int32, shape, 1)
-        high = jnp.where(low == cells - 1, 0, low + 1)
-        value = jnp.where(index == high, frac, 0.0)
-        value = jnp.where(index == low, 1.0 - frac, value)
-        out_ref[rows, :] = value.astype(BF)
+        if not positions_on_lanes:
+            low, high, frac = [
+                jnp.broadcast_to(spot[k : k + 1, rows], (part, part)).T for k in range(3)
+            ]
+            less = 1.0 - frac
+        for j in range(out_ref.shape[1] // part):
+            columns = slice(j * part, (j + 1) * part)
+            if positions_on_lanes:
+                low, high, frac = [spot[k : k + 1, columns] for k in range(3)]
+                less = 1.0 - frac
+                index = lax.broadcasted_iota(jnp.int32, (part, part), 0) + i * part
+            else:
+                index = lax.broadcasted_iota(jnp.int32, (part, part), 1) + j * part
+            index = index.astype(F32)
+            value = jnp.where(index == high, frac, 0.0)
+            value = jnp.where(index == low, less, value)
+            out_ref[rows, columns] = value.astype(BF)
         return carry
 
     lax.fori_loop(0, cells // part, step, 0)
@@ -180,9 +197,9 @@
 
 def middle_kernel(
     count_trans, count_los, length,
-    dens_ref, clow_ref, cfrac_ref, rlow_ref, rfrac_ref, cos_a, sin_a, cos_b, sin_b,
+    slot_ref, dens_ref, row_ref, col_ref, cos_a, sin_a, cos_b, sin_b,
     out_ref, table_out,
-    table, hat, halves, send1, recv1, turned, fields, send2,
+    table, hat, halves, send1, recv1, turned, fields, send2, spot,
     ssem1, rsem1, ssem2, rsem2, lsem,
 ):
     me_t = lax.axis_index("trans")
@@ -217,7 +234,9 @@
     table_copy = pltpu.make_async_copy(table, table_out, lsem.at[0])
     table_copy.start()
 
-    fill_hat(hat, clow_ref, cfrac_ref, True)
+    plane_id = slot_ref[me_l]
+    split_positions(spot, col_ref, plane_id, hat.shape[0])
+    fill_hat(hat, spot, True)
     for c in range(half // chunk):
         low = jnp.dot(dens_ref[...], hat[:, c * chunk : (c + 1) * chunk], preferred_element_type=F32)
         high = jnp.dot(
@@ -226,16 +245,6 @@
         )
         halves[0, :, c * chunk : (c + 1) * chunk] = (low + high).astype(BF)
         halves[1, :, c * chunk : (c + 1) * chunk] = (low - high).astype(BF)
-    for c in range(length // chunk):
-        spec = jnp.dot(
-            halves[c * chunk // half], table[:, c * chunk : (c + 1) * chunk],
-            preferred_element_type=F32,
-        ).astype(BF)
-        for k in range(chunk // lanes):
-            send1[c * (chunk // lanes) + k] = spec[:, k * lanes : (k + 1) * lanes]
-
-    pl.semaphore_wait(barrier, devices - 1)
-
     def copy1(target, source):
         return pltpu.make_async_remote_copy(
             src_ref=send1.at[target], dst_ref=recv1.at[source],
@@ -243,14 +252,31 @@
             device_id=(target, me_l), device_id_type=pl.DeviceIdType.MESH,
         )
 
-    def start1(i, carry):
-        copy1(lax.rem(me_t + i, count_trans), me_t).start()
-        return carry
-
-    lax.fori_loop(1, count_trans, start1, 0)
+    pl.semaphore_wait(barrier, devices - 1)
+    chunks1 = length // chunk
+    per1 = chunk // lanes
+
+    def spectrum_step(i, carry):
+        c = lax.rem(me_t // per1 + chunks1 // 2 + i, chunks1)
+        columns = pl.ds(pl.multiple_of(c * chunk, chunk), chunk)
+        spec = jnp.dot(
+            halves[c // (chunks1 // 2)], table[:, columns], preferred_element_type=F32
+        ).astype(BF)
+        for k in range(per1):
+            target = c * per1 + k
+            send1[target] = spec[:, k * lanes : (k + 1) * lanes]
+
+            @pl.when(target != me_t)
+            def _():
+                copy1(target, me_t).start()
+
+        return carry
+
+    lax.fori_loop(0, chunks1, spectrum_step, 0)
     own1 = pltpu.make_async_copy(send1.at[me_t], recv1.at[me_t], lsem.at[1])
     own1.start()
-    fill_hat(hat, rlow_ref, rfrac_ref, False)
+    split_positions(spot, row_ref, plane_id, hat.shape[1])
+    fill_hat(hat, spot, False)
     own1.wait()
 
     def wait1(i, carry):
@@ -307,24 +333,6 @@
             fields[:lanes, where] = (first + extra).astype(BF)
             fields[lanes:, where] = second.astype(BF)
 
-    contract = (((1,), (1,)), ((), ()))
-    per = chunk // rows_out
-    for c in range(half // chunk):
-        rows = slice(c * chunk, (c + 1) * chunk)
-        part_e = lax.dot_general(
-            table[rows, :half], fields[:, :half], contract, preferred_element_type=F32
-        )
-        part_o = lax.dot_general(
-            table[rows, half:], fields[:, half:], contract, preferred_element_type=F32
-        )
-        for offset, value in ((0, part_e + part_o), (devices // 2, part_e - part_o)):
-            value = value.astype(BF)
-            for k in range(per):
-                for comp in range(2):
-                    send2[offset + c * per + k, comp] = value[
-                        k * rows_out : (k + 1) * rows_out, comp * lanes : (comp + 1) * lanes
-                    ]
-
     def place(other):
         begin = pl.multiple_of((other // count_los) * lanes, lanes)
         return out_ref.at[lax.rem(other, count_los), :, :, pl.ds(begin, lanes)]
@@ -337,11 +345,35 @@
             device_id_type=pl.DeviceIdType.MESH,
         )
 
-    def start2(i, carry):
-        copy2(lax.rem(me + i, devices), me).start()
-        return carry
-
-    lax.fori_loop(1, devices, start2, 0)
+    contract = (((1,), (1,)), ((), ()))
+    per = chunk // rows_out
+    chunks2 = half // chunk
+
+    def back_step(i, carry):
+        c = lax.rem(me // per + chunks2 // 2 + i, chunks2)
+        rows = pl.ds(pl.multiple_of(c * chunk, chunk), chunk)
+        part_e = lax.dot_general(
+            table[rows, :half], fields[:, :half], contract, preferred_element_type=F32
+        )
+        part_o = lax.dot_general(
+            table[rows, half:], fields[:, half:], contract, preferred_element_type=F32
+        )
+        for offset, value in ((0, part_e + part_o), (devices // 2, part_e - part_o)):
+            value = value.astype(BF)
+            for k in range(per):
+                target = offset + c * per + k
+                for comp in range(2):
+                    send2[target, comp] = value[
+                        k * rows_out : (k + 1) * rows_out, comp * lanes : (comp + 1) * lanes
+                    ]
+
+                @pl.when(target != me)
+                def _():
+                    copy2(target, me).start()
+
+        return carry
+
+    lax.fori_loop(0, chunks2, back_step, 0)
     own2 = pltpu.make_async_copy(send2.at[me], place(me), lsem.at[2])
     own2.start()
     own2.wait()
@@ -354,6 +386,58 @@
 
     lax.fori_loop(1, devices, wait2, 0)
     table_copy.wait()
+
+
+def last_kernel(
+    slot_ref, bin_ref, eff_ref, arrived_ref, table_ref, out_ref, whole, sems
+):
+    step = pl.program_id(0)
+    planes, comps, rows, length = arrived_ref.shape
+    half = length // 2
+    bins = eff_ref.shape[0]
+    chunk = table_ref.shape[0]
+    contract = (((1,), (1,)), ((), ()))
+    values = arrived_ref[...].reshape(planes * comps * rows, length)
+    part_e = lax.dot_general(
+        values[:, :half], table_ref[:, :half], contract, preferred_element_type=F32
+    )
+    part_o = lax.dot_general(
+        values[:, half:], table_ref[:, half:], contract, preferred_element_type=F32
+    )
+    sides = (part_e + part_o, part_e - part_o)
+    weights = []
+    for b in range(bins):
+        row = []
+        for slot in range(planes):
+            plane = slot_ref[slot]
+            row.append(jnp.where(b >= bin_ref[plane], eff_ref[b, plane], 0.0))
+        weights.append(row)
+
+    def out_copy(at, side):
+        columns = pl.ds(pl.multiple_of(side * half + at * chunk, chunk), chunk)
+        return pltpu.make_async_copy(
+            whole.at[:, :, :, columns], out_ref.at[:, :, :, columns], sems.at[at, side]
+        )
+
+    for side in range(2):
+        columns = pl.ds(pl.multiple_of(side * half + step * chunk, chunk), chunk)
+        for comp in range(comps):
+            maps = [
+                sides[side][(slot * comps + comp) * rows : (slot * comps + comp + 1) * rows]
+                for slot in range(planes)
+            ]
+            for b in range(bins):
+                total = weights[b][0] * maps[0]
+                for slot in range(1, planes):
+                    total = total + weights[b][slot] * maps[slot]
+                whole[comp, b, :, columns] = total
+        out_copy(step, side).start()
+
+    @pl.when(step == half // chunk - 1)
+    def _():
+        for at in range(half // chunk):
+            for side in range(2):
+                out_copy(at, side).wait()
 
 
 def body_kernel(density, row_pos, col_pos, plane_of_slot, plane_bin, efficiency):
@@ -364,31 +448,20 @@
     half = length // 2
     width = half // count_trans
     lanes = 2 * width
-    planes = row_pos.shape[0]
     bins = efficiency.shape[0]
     devices = count_trans * count_los
     rows_out = length // devices
 
-    slots = jnp.arange(planes, dtype=jnp.int32)
-    plane_id = jnp.sum(jnp.where(slots == lax.axis_index("los"), plane_of_slot, 0))
-
-    def split(positions):
-        here = jnp.sum(jnp.where((slots == plane_id)[:, None], positions, 0.0), axis=0)
-        base = jnp.floor(here)
-        low = base.astype(jnp.int32)
-        return jnp.where(low >= cells, low - cells, low), here - base
-
-    clow, cfrac = split(col_pos)
-    rlow, rfrac = split(row_pos)
     tables = [jnp.asarray(t) for t in small_tables(length, width)]
     vmem = pl.BlockSpec(memory_space=pltpu.VMEM)
+    smem = pl.BlockSpec(memory_space=pltpu.SMEM)
     arrived, table = pl.pallas_call(
         functools.partial(middle_kernel, count_trans, count_los, length),
         out_shape=[
             jax.ShapeDtypeStruct((count_los, 2, rows_out, length), BF),
             jax.ShapeDtypeStruct((half, length), BF),
         ],
-        in_specs=[vmem] * 9,
+        in_specs=[smem] + [vmem] * 7,
         out_specs=[vmem, pl.BlockSpec(memory_space=pl.ANY)],
         scratch_shapes=[
             pltpu.VMEM((half, length), BF),
@@ -399,6 +472,7 @@
             pltpu.VMEM((2, lanes, half), BF),
             pltpu.VMEM((2 * lanes, length), BF),
             pltpu.VMEM((devices, 2, rows_out, lanes), BF),
+            pltpu.VMEM((8, length), F32),
             pltpu.SemaphoreType.DMA((count_trans,)),
             pltpu.SemaphoreType.DMA((count_trans,)),
             pltpu.SemaphoreType.DMA((devices,)),
@@ -408,22 +482,24 @@
         compiler_params=pltpu.CompilerParams(
             collective_id=0, has_side_effects=True, vmem_limit_bytes=56 * 1024 * 1024
         ),
-    )(
-        density[0], clow[None, :], cfrac[None, :], rlow[:, None], rfrac[:, None], *tables
-    )
-    arrived = arrived.reshape(count_los * 2 * rows_out, length)
-    part_e = dot(arrived[:, :half], table[:, :half], ((1,), (1,)))
-    part_o = dot(arrived[:, half:], table[:, half:], ((1,), (1,)))
-    maps = jnp.concatenate([part_e + part_o, part_e - part_o], axis=1)
-    maps = maps.reshape(count_los, 2, rows_out, length)
-    total = 0.0
-    for slot in range(planes):
-        chosen = slots == plane_of_slot[slot]
-        slot_eff = jnp.sum(jnp.where(chosen[None, :], efficiency, 0.0), axis=1)
-        first_bin = jnp.sum(jnp.where(chosen, plane_bin, 0))
-        weight = jnp.where(jnp.arange(bins) >= first_bin, slot_eff, 0.0)
-        total = total + weight[None, :, None, None] * maps[slot][:, None]
-    return total
+    )(plane_of_slot, density[0], row_pos, col_pos, *tables)
+    chunk = 256
+    return pl.pallas_call(
+        last_kernel,
+        grid=(half // chunk,),
+        out_shape=jax.ShapeDtypeStruct((2, bins, rows_out, length), F32),
+        in_specs=[smem] * 3
+        + [
+            pl.BlockSpec((count_los, 2, rows_out, length), lambda i: (0, 0, 0, 0)),
+            pl.BlockSpec((chunk, length), lambda i: (i, 0)),
+        ],
+        out_specs=pl.BlockSpec(memory_space=pl.ANY),
+        scratch_shapes=[
+            pltpu.VMEM((2, bins, rows_out, length), F32),
+            pltpu.SemaphoreType.DMA((half // chunk, 2)),
+        ],
+        compiler_params=pltpu.CompilerParams(vmem_limit_bytes=32 * 1024 * 1024),
+    )(plane_of_slot, plane_bin, efficiency, arrived, table)
 
 
 def body(density, row_pos, *rest):

time: 71.9 us -> 61.8 us (0.86)
  the two profiles are of different devices: /device:TPU:15 before, /device:TPU:11 now
where the time goes in v3:
time: 61.8 us; the launch traced here: 61.6 us
  Pallas kernels  56.1 us (91%)
  local copies, waits for them, and re-layouts  5.48 us (9%)
    pallas_call x1, Pallas kernels, body_kernel(): pl.pallas_call(functools.partial(middle_kernel, count_trans, count_los, l...  52 us
    unnamed x9, local copies, waits for them, and re-layouts  5.48 us
    pallas_call x1, Pallas kernels, body_kernel(): pl.pallas_call(last_kernel, grid=(half // chunk,), out_shape=jax.ShapeDty...  4.05 us

profile of v3, /device:TPU:11, one launch (start us, length us, event | category | flops | bytes accessed | tf_op | source)
XLA Modules:
  0.0 61.6 jit_solution(6898673815153289546)
XLA Ops:
  0.0 0.8 %copy.11.eff_ref = f32[4,2]{1,0:T(4,128)S(1)} copy(f32[4,2]{0,1:T(2,128)} %param.15) | data formatting | bytes 64 | tf_op args[5]
  0.8 52.0 %shard_map.100 = (bf16[2,2,64,2048]{3,2,1,0:T(8,128)(2,1)}, bf16[1024,2048]{1,0:T(8,128)(2,1)}) custom-call(s32[2]{0:T(128)} %slot_ref.3, bf16[128,2048]{1,0:T(8,128)(2,1)} %bitcast.1, f32[2,2048]{1,0:T(2,128)} %row_ref.1, f32[2,2048]{1,0:T(2,128)} %col_ref.1, f32[32,2048]{1,0:T(8,128)} %constant.8.clone.cos_a, f32[32,2048]{1,0:T(8,128)} %constant.9.clone.sin_a, ...), custom_call_target="tpu_custom_call" | custom-call | tf_op jit(solution)/shard_map/pallas_call | solution.py:458
  52.8 0.0 copy-start
  52.8 2.2 %copy-done = bf16[1024,2048]{1,0:T(8,128)(2,1)S(1)} copy-done((bf16[1024,2048]{1,0:T(8,128)(2,1)S(1)}, bf16[1024,2048]{1,0:T(8,128)(2,1)}, u32[]{:S(2)}) %copy-start) | copy-done | bytes 4194328
  55.0 0.0 copy-start.1
  55.0 1.2 %copy-done.1 = bf16[2,2,64,2048]{3,2,1,0:T(8,128)(2,1)S(1)} copy-done((bf16[2,2,64,2048]{3,2,1,0:T(8,128)(2,1)S(1)}, bf16[2,2,64,2048]{3,2,1,0:T(8,128)(2,1)}, u32[]{:S(2)}) %copy-start.1) | copy-done | bytes 1048600
  56.2 0.0 copy-start.2
  56.2 0.7 %copy-done.2 = s32[2]{0:T(128)S(1)} copy-done((s32[2]{0:T(128)S(1)}, s32[2]{0:T(128)}, u32[]{:S(2)}) %copy-start.2) | copy-done | bytes 32
  56.9 0.0 copy-start.3
  56.9 0.7 %copy-done.3 = s32[2]{0:T(128)S(1)} copy-done((s32[2]{0:T(128)S(1)}, s32[2]{0:T(128)}, u32[]{:S(2)}) %copy-start.3) | copy-done | bytes 32
  57.5 4.0 %shard_map.101 = f32[2,4,64,2048]{3,2,1,0:T(8,128)} custom-call(s32[2]{0:T(128)S(1)} %copy-done.2, s32[2]{0:T(128)S(1)} %copy-done.3, f32[4,2]{1,0:T(4,128)S(1)} %copy.11.eff_ref, bf16[2,2,64,2048]{3,2,1,0:T(8,128)(2,1)S(1)} %copy-done.1, bf16[1024,2048]{1,0:T(8,128)(2,1)S(1)} %copy-done), custom_call_target="tpu_custom_call" | custom-call | tf_op jit(solution)/shard_map/pallas_call | solution.py:487
Async XLA Ops:
  52.8 2.2 %copy-start = (bf16[1024,2048]{1,0:T(8,128)(2,1)S(1)}, bf16[1024,2048]{1,0:T(8,128)(2,1)}, u32[]{:S(2)}) copy-start(bf16[1024,2048]{1,0:T(8,128)(2,1)} %get-tuple-element.8.table_ref) | copy-start | bytes 12582916
  55.0 1.2 %copy-start.1 = (bf16[2,2,64,2048]{3,2,1,0:T(8,128)(2,1)S(1)}, bf16[2,2,64,2048]{3,2,1,0:T(8,128)(2,1)}, u32[]{:S(2)}) copy-start(bf16[2,2,64,2048]{3,2,1,0:T(8,128)(2,1)} %get-tuple-element.7.arrived_ref) | copy-start | bytes 3145732
  56.2 0.7 %copy-start.2 = (s32[2]{0:T(128)S(1)}, s32[2]{0:T(128)}, u32[]{:S(2)}) copy-start(s32[2]{0:T(128)} %slot_ref.3) | copy-start | bytes 28
  56.9 0.7 %copy-start.3 = (s32[2]{0:T(128)S(1)}, s32[2]{0:T(128)}, u32[]{:S(2)}) copy-start(s32[2]{0:T(128)} %bin_ref.1) | copy-start | bytes 28

commit v4 on v3

--- a/solution.py
+++ b/solution.py
@@ -185,7 +185,10 @@
                 less = 1.0 - frac
                 index = lax.broadcasted_iota(jnp.int32, (part, part), 0) + i * part
             else:
-                index = lax.broadcasted_iota(jnp.int32, (part, part), 1) + j * part
+                lane = lax.broadcasted_iota(jnp.int32, (part, part), 1)
+                count = out_ref.shape[1] // part // 2
+                start = 2 * (j % count) * part + (part // 2) * (j // count)
+                index = lane + jnp.where(lane >= part // 2, part // 2, 0) + start
             index = index.astype(F32)
             value = jnp.where(index == high, frac, 0.0)
             value = jnp.where(index == low, less, value)
@@ -197,17 +200,25 @@
 
 def middle_kernel(
     count_trans, count_los, length,
-    slot_ref, dens_ref, row_ref, col_ref, cos_a, sin_a, cos_b, sin_b,
-    out_ref, table_out,
-    table, hat, halves, send1, recv1, turned, fields, send2, spot,
-    ssem1, rsem1, ssem2, rsem2, lsem,
+    slot_ref, row_ref, col_ref, dens_hbm, *refs
 ):
+    small_hbm, refs = refs[:4], refs[4:]
+    out_ref, table, hat, halves, send1, recv1, turned, fields, send2 = refs[:9]
+    spot, dens_ref, cos_a, sin_a, cos_b, sin_b, ssem1, rsem1, ssem2, rsem2, lsem = refs[9:]
+    loads = [
+        pltpu.make_async_copy(source, target, lsem.at[3 + k])
+        for k, (source, target) in enumerate(
+            zip((dens_hbm, *small_hbm), (dens_ref, cos_a, sin_a, cos_b, sin_b))
+        )
+    ]
+    for load in loads:
+        load.start()
     me_t = lax.axis_index("trans")
     me_l = lax.axis_index("los")
     devices = count_trans * count_los
     me = me_t * count_los + me_l
     half = length // 2
-    width = half // count_trans
+    width = half // count_trans // 2
     lanes = 2 * width
     rows_out = length // devices
     chunk = 256
@@ -224,6 +235,12 @@
 
     lax.fori_loop(1, devices, greet, 0)
 
+    plane_id = slot_ref[me_l]
+    split_positions(spot, col_ref, plane_id, hat.shape[0])
+    fill_hat(hat, spot, True)
+    for load in loads:
+        load.wait()
+
     def table_step(i, carry):
         rows = pl.ds(pl.multiple_of(i * STEP, STEP), STEP)
         value = cos_a[pl.ds(i, 1), :] * cos_b[...] - sin_a[pl.ds(i, 1), :] * sin_b[...]
@@ -231,12 +248,7 @@
         return carry
 
     lax.fori_loop(0, half // STEP, table_step, 0)
-    table_copy = pltpu.make_async_copy(table, table_out, lsem.at[0])
-    table_copy.start()
-
-    plane_id = slot_ref[me_l]
-    split_positions(spot, col_ref, plane_id, hat.shape[0])
-    fill_hat(hat, spot, True)
+
     for c in range(half // chunk):
         low = jnp.dot(dens_ref[...], hat[:, c * chunk : (c + 1) * chunk], preferred_element_type=F32)
         high = jnp.dot(
@@ -245,164 +257,208 @@
         )
         halves[0, :, c * chunk : (c + 1) * chunk] = (low + high).astype(BF)
         halves[1, :, c * chunk : (c + 1) * chunk] = (low - high).astype(BF)
-    def copy1(target, source):
+    def copy1(parity, target, source):
         return pltpu.make_async_remote_copy(
-            src_ref=send1.at[target], dst_ref=recv1.at[source],
-            send_sem=ssem1.at[target], recv_sem=rsem1.at[source],
+            src_ref=send1.at[parity, target], dst_ref=recv1.at[parity, source],
+            send_sem=ssem1.at[parity, target], recv_sem=rsem1.at[parity, source],
             device_id=(target, me_l), device_id_type=pl.DeviceIdType.MESH,
         )
 
     pl.semaphore_wait(barrier, devices - 1)
-    chunks1 = length // chunk
+    chunks1 = half // chunk
     per1 = chunk // lanes
-
-    def spectrum_step(i, carry):
-        c = lax.rem(me_t // per1 + chunks1 // 2 + i, chunks1)
-        columns = pl.ds(pl.multiple_of(c * chunk, chunk), chunk)
-        spec = jnp.dot(
-            halves[c // (chunks1 // 2)], table[:, columns], preferred_element_type=F32
-        ).astype(BF)
-        for k in range(per1):
-            target = c * per1 + k
-            send1[target] = spec[:, k * lanes : (k + 1) * lanes]
-
-            @pl.when(target != me_t)
-            def _():
-                copy1(target, me_t).start()
-
-        return carry
-
-    lax.fori_loop(0, chunks1, spectrum_step, 0)
-    own1 = pltpu.make_async_copy(send1.at[me_t], recv1.at[me_t], lsem.at[1])
-    own1.start()
+    rows_half = send1.shape[2]
+    owns = []
+    for parity in range(2):
+
+        def spectrum_step(i, carry):
+            c = lax.rem(me_t // per1 + chunks1 // 2 + i, chunks1)
+            columns = pl.ds(pl.multiple_of(parity * half + c * chunk, chunk), chunk)
+            spec = jnp.dot(halves[parity], table[:, columns], preferred_element_type=F32)
+            for k in range(per1):
+                target = c * per1 + k
+                block = spec[:, k * lanes : (k + 1) * lanes]
+                send1[parity, target] = jnp.concatenate(
+                    [block[:rows_half], block[rows_half:]], axis=1
+                ).astype(BF)
+
+                @pl.when(target != me_t)
+                def _():
+                    copy1(parity, target, me_t).start()
+
+            return carry
+
+        lax.fori_loop(0, chunks1, spectrum_step, 0)
+        owns.append(
+            pltpu.make_async_copy(
+                send1.at[parity, me_t], recv1.at[parity, me_t], lsem.at[parity]
+            )
+        )
+        owns[parity].start()
     split_positions(spot, row_ref, plane_id, hat.shape[1])
     fill_hat(hat, spot, False)
-    own1.wait()
-
-    def wait1(i, carry):
-        other = lax.rem(me_t + i, count_trans)
-        copy1(other, me_t).wait_send()
-        copy1(me_t, other).wait_recv()
-        return carry
-
-    lax.fori_loop(1, count_trans, wait1, 0)
-
-    columns = recv1[...].reshape(hat.shape[1], lanes)
-    for c in range(half // chunk):
-        low = jnp.dot(hat[c * chunk : (c + 1) * chunk, :], columns, preferred_element_type=F32)
-        high = jnp.dot(
-            hat[half + c * chunk : half + (c + 1) * chunk, :], columns,
-            preferred_element_type=F32,
-        )
-        turned[0, :, c * chunk : (c + 1) * chunk] = (low + high).T.astype(BF)
-        turned[1, :, c * chunk : (c + 1) * chunk] = (low - high).T.astype(BF)
-
-    shape = (lanes, lanes)
-    k2, lane_nyq, lane_sine, lane_end = fold_waves(
-        length, width, me_t, lax.broadcasted_iota(jnp.int32, shape, 0)
-    )
-    lane_sign = jnp.where(lane_sine, 1.0, -1.0)
-    scale2 = jnp.where(lane_end | lane_nyq, 1.0, 2.0) * (1.0 / length)
+
+    def place(parity, other):
+        begin = pl.multiple_of((other // count_los) * 2 * lanes, 2 * lanes)
+        return out_ref.at[parity, lax.rem(other, count_los), :, pl.ds(begin, 2 * lanes)]
+
+    def copy2(parity, target, source):
+        return pltpu.make_async_remote_copy(
+            src_ref=send2.at[parity, target], dst_ref=place(parity, source),
+            send_sem=ssem2.at[parity, target], recv_sem=rsem2.at[parity, source],
+            device_id=(target // count_los, lax.rem(target, count_los)),
+            device_id_type=pl.DeviceIdType.MESH,
+        )
+
+    contract = (((1,), (1,)), ((), ()))
+    per = chunk // rows_out
+    chunks2 = half // chunk
+    shape = (lanes, chunk)
     inner = lax.broadcasted_iota(jnp.int32, shape, 1)
-    for c in range(length // chunk):
-        freq2 = jnp.dot(
-            turned[c * chunk // half], table[:, c * chunk : (c + 1) * chunk],
-            preferred_element_type=F32,
-        )
-        for k in range(chunk // lanes):
-            block = c * (chunk // lanes) + k
-            freq = freq2[:, k * lanes : (k + 1) * lanes]
-            k1, row_nyq, row_sine, row_end = fold_waves(length, width, jnp.int32(block), inner)
+    member = jnp.bitwise_and(inner, lanes - 1)
+    for parity in range(2):
+        owns[parity].wait()
+
+        def wait1(i, carry):
+            other = lax.rem(me_t + i, count_trans)
+            copy1(parity, other, me_t).wait_send()
+            copy1(parity, me_t, other).wait_recv()
+            return carry
+
+        lax.fori_loop(1, count_trans, wait1, 0)
+        columns = recv1[parity].reshape(half, 2 * lanes)
+
+        def resample(begin):
+            rows = slice(begin, begin + chunk)
+            one = jnp.dot(hat[rows, :half], columns, preferred_element_type=F32)
+            two = jnp.dot(hat[rows, half:], columns, preferred_element_type=F32)
+            return one + pltpu.roll(two, lanes, 1)
+
+        for c in range(half // chunk):
+            low = resample(c * chunk)
+            high = resample(half + c * chunk)
+            turned[0, :, c * chunk : (c + 1) * chunk] = (low + high).T[:lanes].astype(BF)
+            turned[1, :, c * chunk : (c + 1) * chunk] = (low - high).T[:lanes].astype(BF)
+
+        k2, lane_nyq, lane_sine, lane_end = fold_waves(
+            length, width, parity * count_trans + me_t,
+            lax.broadcasted_iota(jnp.int32, shape, 0),
+        )
+        lane_sign = jnp.where(lane_sine, 1.0, -1.0)
+        scale2 = jnp.where(lane_end | lane_nyq, 1.0, 2.0) * (1.0 / length)
+
+        def swap(value):
+            ahead = pltpu.roll(value, chunk - width, 1)
+            return jnp.where(member < width, ahead, pltpu.roll(value, width, 1))
+
+        for c in range(length // chunk):
+            where = slice(c * chunk, (c + 1) * chunk)
+            freq = jnp.dot(
+                turned[c // chunks2], table[:, where], preferred_element_type=F32
+            )
+            block = c * (chunk // lanes) + lax.div(inner, lanes)
+            k1, row_nyq, row_sine, row_end = fold_waves(length, width, block, member)
             row_sign = jnp.where(row_sine, 1.0, -1.0)
             scale1 = jnp.where(row_end | row_nyq, 1.0, 2.0) * (1.0 / length)
             scale = scale1 * scale2 / jnp.maximum(k1 * k1 + k2 * k2, 1.0)
             d1 = (k1 * k1 - k2 * k2) * scale
             d2 = 2.0 * k1 * k2 * scale
-            swap_rows = pltpu.roll(freq, width, 1)
             swap_lanes = jnp.concatenate([freq[width:], freq[:width]], axis=0)
-            swap_both = pltpu.roll(swap_lanes, width, 1)
+            swap_both = swap(swap_lanes)
             first = d1 * freq
-            extra = jnp.where(lane_nyq, row_sign * d2 * swap_rows, 0.0)
-            second = jnp.where(lane_nyq, 0.0, -row_sign * lane_sign * d2 * swap_both)
-            if block == 0:
+            second = -row_sign * lane_sign * d2 * swap_both
+            if parity == 0:
+                extra = jnp.where(lane_nyq, row_sign * d2 * swap(freq), 0.0)
+                second = jnp.where(lane_nyq, 0.0, second)
+            else:
+                extra = jnp.zeros_like(freq)
+            if c == 0:
                 extra = jnp.where(
                     row_nyq, jnp.where(lane_nyq, 0.0, lane_sign * d2 * swap_lanes), extra
                 )
                 second = jnp.where(row_nyq, jnp.where(lane_nyq, d2 * freq, 0.0), second)
-            where = slice(block * lanes, (block + 1) * lanes)
             fields[:lanes, where] = (first + extra).astype(BF)
             fields[lanes:, where] = second.astype(BF)
 
-    def place(other):
-        begin = pl.multiple_of((other // count_los) * lanes, lanes)
-        return out_ref.at[lax.rem(other, count_los), :, :, pl.ds(begin, lanes)]
-
-    def copy2(target, source):
-        return pltpu.make_async_remote_copy(
-            src_ref=send2.at[target], dst_ref=place(source),
-            send_sem=ssem2.at[target], recv_sem=rsem2.at[source],
-            device_id=(target // count_los, lax.rem(target, count_los)),
-            device_id_type=pl.DeviceIdType.MESH,
-        )
-
-    contract = (((1,), (1,)), ((), ()))
-    per = chunk // rows_out
-    chunks2 = half // chunk
-
-    def back_step(i, carry):
-        c = lax.rem(me // per + chunks2 // 2 + i, chunks2)
-        rows = pl.ds(pl.multiple_of(c * chunk, chunk), chunk)
-        part_e = lax.dot_general(
-            table[rows, :half], fields[:, :half], contract, preferred_element_type=F32
-        )
-        part_o = lax.dot_general(
-            table[rows, half:], fields[:, half:], contract, preferred_element_type=F32
-        )
-        for offset, value in ((0, part_e + part_o), (devices // 2, part_e - part_o)):
-            value = value.astype(BF)
-            for k in range(per):
-                target = offset + c * per + k
-                for comp in range(2):
-                    send2[target, comp] = value[
-                        k * rows_out : (k + 1) * rows_out, comp * lanes : (comp + 1) * lanes
-                    ]
-
-                @pl.when(target != me)
-                def _():
-                    copy2(target, me).start()
-
-        return carry
-
-    lax.fori_loop(0, chunks2, back_step, 0)
-    own2 = pltpu.make_async_copy(send2.at[me], place(me), lsem.at[2])
-    own2.start()
-    own2.wait()
-
-    def wait2(i, carry):
-        other = lax.rem(me + i, devices)
-        copy2(other, me).wait_send()
-        copy2(me, other).wait_recv()
-        return carry
-
-    lax.fori_loop(1, devices, wait2, 0)
-    table_copy.wait()
+        def back_step(i, carry):
+            c = lax.rem(me // per + chunks2 // 2 + i, chunks2)
+            rows = pl.ds(pl.multiple_of(c * chunk, chunk), chunk)
+            part_e = lax.dot_general(
+                table[rows, :half], fields[:, :half], contract, preferred_element_type=F32
+            )
+            part_o = lax.dot_general(
+                table[rows, half:], fields[:, half:], contract, preferred_element_type=F32
+            )
+            for offset, value in ((0, part_e + part_o), (devices // 2, part_e - part_o)):
+                value = value.astype(BF)
+                for k in range(per):
+                    target = offset + c * per + k
+                    send2[parity, target] = value[k * rows_out : (k + 1) * rows_out]
+
+                    @pl.when(target != me)
+                    def _():
+                        copy2(parity, target, me).start()
+
+            return carry
+
+        lax.fori_loop(0, chunks2, back_step, 0)
+        own2 = pltpu.make_async_copy(send2.at[parity, me], place(parity, me), lsem.at[2])
+        own2.start()
+        own2.wait()
+
+    for parity in range(2):
+
+        def wait2(i, carry):
+            other = lax.rem(me + i, devices)
+            copy2(parity, other, me).wait_send()
+            copy2(parity, me, other).wait_recv()
+            return carry
+
+        lax.fori_loop(1, devices, wait2, 0)
 
 
 def last_kernel(
-    slot_ref, bin_ref, eff_ref, arrived_ref, table_ref, out_ref, whole, sems
+    slot_ref, bin_ref, eff_ref, arrived_ref, cos_a, sin_a, cos_b, sin_b, out_ref,
+    whole, values, table, sems,
 ):
     step = pl.program_id(0)
-    planes, comps, rows, length = arrived_ref.shape
-    half = length // 2
-    bins = eff_ref.shape[0]
-    chunk = table_ref.shape[0]
+    comps = 2
+    planes, rows, length = arrived_ref.shape[1:]
+    half = length // 2
+    bins = eff_ref.shape[1]
+    chunk = table.shape[0]
     contract = (((1,), (1,)), ((), ()))
-    values = arrived_ref[...].reshape(planes * comps * rows, length)
+
+    @pl.when(step == 0)
+    def _():
+        tile = 128
+        first = lax.broadcasted_iota(jnp.int32, (rows, tile), 1) < tile // 2
+        for parity in range(2):
+            for slot in range(planes):
+                for pair in range(half // tile):
+                    left, right = [
+                        arrived_ref[
+                            parity, slot, :, (2 * pair + k) * tile : (2 * pair + k + 1) * tile
+                        ].astype(F32)
+                        for k in range(2)
+                    ]
+                    zero = jnp.where(first, left, pltpu.roll(right, tile // 2, 1))
+                    one = jnp.where(first, pltpu.roll(left, tile // 2, 1), right)
+                    for comp, value in enumerate((zero, one)):
+                        begin = (slot * comps + comp) * rows
+                        values[
+                            parity, begin : begin + rows, pair * tile : (pair + 1) * tile
+                        ] = value.astype(BF)
+
+    for k in range(chunk // STEP):
+        at = step * (chunk // STEP) + k
+        value = cos_a[pl.ds(at, 1), :] * cos_b[...] - sin_a[pl.ds(at, 1), :] * sin_b[...]
+        table[k * STEP : (k + 1) * STEP, :] = value.astype(BF)
     part_e = lax.dot_general(
-        values[:, :half], table_ref[:, :half], contract, preferred_element_type=F32
+        values[0], table[:, :half], contract, preferred_element_type=F32
     )
     part_o = lax.dot_general(
-        values[:, half:], table_ref[:, half:], contract, preferred_element_type=F32
+        values[1], table[:, half:], contract, preferred_element_type=F32
     )
     sides = (part_e + part_o, part_e - part_o)
     weights = []
@@ -410,7 +466,7 @@
         row = []
         for slot in range(planes):
             plane = slot_ref[slot]
-            row.append(jnp.where(b >= bin_ref[plane], eff_ref[b, plane], 0.0))
+            row.append(jnp.where(b >= bin_ref[plane], eff_ref[plane, b], 0.0))
         weights.append(row)
 
     def out_copy(at, side):
@@ -446,7 +502,7 @@
     rows_in, cells = density.shape[1:]
     length = row_pos.shape[1]
     half = length // 2
-    width = half // count_trans
+    width = half // count_trans // 2
     lanes = 2 * width
     bins = efficiency.shape[0]
     devices = count_trans * count_los
@@ -455,34 +511,33 @@
     tables = [jnp.asarray(t) for t in small_tables(length, width)]
     vmem = pl.BlockSpec(memory_space=pltpu.VMEM)
     smem = pl.BlockSpec(memory_space=pltpu.SMEM)
-    arrived, table = pl.pallas_call(
+    arrived = pl.pallas_call(
         functools.partial(middle_kernel, count_trans, count_los, length),
-        out_shape=[
-            jax.ShapeDtypeStruct((count_los, 2, rows_out, length), BF),
-            jax.ShapeDtypeStruct((half, length), BF),
-        ],
-        in_specs=[smem] + [vmem] * 7,
-        out_specs=[vmem, pl.BlockSpec(memory_space=pl.ANY)],
+        out_shape=jax.ShapeDtypeStruct((2, count_los, rows_out, 2 * lanes * count_trans), BF),
+        in_specs=[smem] + [vmem] * 2 + [pl.BlockSpec(memory_space=pltpu.HBM)] * 5,
+        out_specs=vmem,
         scratch_shapes=[
             pltpu.VMEM((half, length), BF),
             pltpu.VMEM((length, cells), BF),
             pltpu.VMEM((2, rows_in, half), BF),
-            pltpu.VMEM((count_trans, rows_in, lanes), BF),
-            pltpu.VMEM((count_trans, rows_in, lanes), BF),
+            pltpu.VMEM((2, count_trans, rows_in // 2, 2 * lanes), BF),
+            pltpu.VMEM((2, count_trans, rows_in // 2, 2 * lanes), BF),
             pltpu.VMEM((2, lanes, half), BF),
             pltpu.VMEM((2 * lanes, length), BF),
-            pltpu.VMEM((devices, 2, rows_out, lanes), BF),
+            pltpu.VMEM((2, devices, rows_out, 2 * lanes), BF),
             pltpu.VMEM((8, length), F32),
-            pltpu.SemaphoreType.DMA((count_trans,)),
-            pltpu.SemaphoreType.DMA((count_trans,)),
-            pltpu.SemaphoreType.DMA((devices,)),
-            pltpu.SemaphoreType.DMA((devices,)),
-            pltpu.SemaphoreType.DMA((3,)),
+            pltpu.VMEM((rows_in, cells), BF),
+            *[pltpu.VMEM(t.shape, F32) for t in tables],
+            pltpu.SemaphoreType.DMA((2, count_trans)),
+            pltpu.SemaphoreType.DMA((2, count_trans)),
+            pltpu.SemaphoreType.DMA((2, devices)),
+            pltpu.SemaphoreType.DMA((2, devices)),
+            pltpu.SemaphoreType.DMA((8,)),
         ],
         compiler_params=pltpu.CompilerParams(
-            collective_id=0, has_side_effects=True, vmem_limit_bytes=56 * 1024 * 1024
+            collective_id=0, has_side_effects=True, vmem_limit_bytes=63 * 1024 * 1024
         ),
-    )(plane_of_slot, density[0], row_pos, col_pos, *tables)
+    )(plane_of_slot, row_pos, col_pos, density[0], *tables)
     chunk = 256
     return pl.pallas_call(
         last_kernel,
@@ -490,16 +545,18 @@
         out_shape=jax.ShapeDtypeStruct((2, bins, rows_out, length), F32),
         in_specs=[smem] * 3
         + [
-            pl.BlockSpec((count_los, 2, rows_out, length), lambda i: (0, 0, 0, 0)),
-            pl.BlockSpec((chunk, length), lambda i: (i, 0)),
+            pl.BlockSpec(arrived.shape, lambda i: (0, 0, 0, 0)),
+            *[pl.BlockSpec(t.shape, lambda i: (0, 0)) for t in tables],
         ],
         out_specs=pl.BlockSpec(memory_space=pl.ANY),
         scratch_shapes=[
             pltpu.VMEM((2, bins, rows_out, length), F32),
+            pltpu.VMEM((2, count_los * 2 * rows_out, half), BF),
+            pltpu.VMEM((chunk, length), BF),
             pltpu.SemaphoreType.DMA((half // chunk, 2)),
         ],
-        compiler_params=pltpu.CompilerParams(vmem_limit_bytes=32 * 1024 * 1024),
-    )(plane_of_slot, plane_bin, efficiency, arrived, table)
+        compiler_params=pltpu.CompilerParams(vmem_limit_bytes=63 * 1024 * 1024),
+    )(plane_of_slot, plane_bin, efficiency.T, arrived, *tables)
 
 
 def body(density, row_pos, *rest):

time: 61.8 us -> 54.7 us (0.89)
  the two profiles are of different devices: /device:TPU:11 before, /device:TPU:0 now
where the time goes in v4:
time: 54.7 us; the launch traced here: 54.1 us
  Pallas kernels  54 us (99%)
    pallas_call x1, Pallas kernels, body_kernel(): pl.pallas_call(functools.partial(middle_kernel, count_trans, count_los, l...  48.4 us
    pallas_call x1, Pallas kernels, body_kernel(): pl.pallas_call(last_kernel, grid=(half // chunk,), out_shape=jax.ShapeDty...  5.69 us

profile of v4, /device:TPU:0, one launch (start us, length us, event | category | flops | bytes accessed | tf_op | source)
XLA Modules:
  0.0 54.1 jit_solution(4412160139734582029)
XLA Ops:
  0.0 48.4 %shard_map.100.arrived_ref = bf16[2,2,64,2048]{3,2,1,0:T(8,128)(2,1)} custom-call(s32[2]{0:T(128)} %slot_ref.3, f32[2,2048]{1,0:T(2,128)} %row_ref.1, f32[2,2048]{1,0:T(2,128)} %col_ref.1, bf16[128,2048]{1,0:T(8,128)(2,1)} %bitcast.2, f32[32,2048]{1,0:T(8,128)} %constant.8.clone.refs_0_.cos_a, f32[32,2048]{1,0:T(8,128)} %constant.9.clone.refs_1_.sin_a, ...), custom_call_target="tpu_custom_call" | custom-call | tf_op jit(solution)/shard_map/pallas_call | solution.py:514
  48.4 5.7 %shard_map.101 = f32[2,4,64,2048]{3,2,1,0:T(8,128)} custom-call(s32[2]{0:T(128)} %slot_ref.3, s32[2]{0:T(128)} %bin_ref.1, f32[2,4]{1,0:T(2,128)} %bitcast.3, bf16[2,2,64,2048]{3,2,1,0:T(8,128)(2,1)} %shard_map.100.arrived_ref, f32[32,2048]{1,0:T(8,128)} %constant.8.clone.refs_0_.cos_a, f32[32,2048]{1,0:T(8,128)} %constant.9.clone.refs_1_.sin_a, ...), custom_call_target="tpu_custom_call" | custom-call | tf_op jit(solution)/shard_map/pallas_call | solution.py:542
